TPU v7x, 8 devices: a whole 2x2x1 slice. The times are simulated.
8 devices in a mesh: spin: 1 (over z), depth: 2 (over y), row: 2 (over x), col: 2 (over core).
Axes of the slice: x: 2, y: 2, z: 1, core: 2. Of those that a mesh axis runs over, the one named last changes fastest.
Arguments:
- hamiltonian: float32 [16, 1536, 1536], P('spin', 'row', 'col')
- spec_bounds: float32 [16, 2], P('spin')
- occ_count: int32 [16], P('spin')
Outputs:
- output 1: float32 [16, 1536, 1536], P('spin', 'row', 'col')
- output 2: float32 [16], P('spin')
All inputs are finite; a program needn't handle non-finite values.
Results may differ from a plain program's by a relative error of at most 0.001.
Values sent between devices are 32-bit elements.
A program may use at most 1 GiB of HBM per device.

v0:
```python
import jax
import jax.numpy as jnp
from jax import lax
from jax.sharding import PartitionSpec as P

STEPS = 3


def solution(mesh):
    depth_size = mesh.shape['depth']
    row_size = mesh.shape['row']
    col_size = mesh.shape['col']
    per_col = row_size // col_size
    highest = lax.Precision.HIGHEST

    def local_purify(ham_blk, spec_bounds, occ_count):
        kpoints, row_blk, col_blk = ham_blk.shape
        mat_order = col_blk * col_size
        sub_width = row_blk // depth_size
        row_idx = lax.axis_index('row')
        col_idx = lax.axis_index('col')
        layer_idx = lax.axis_index('depth')
        on_diag = (row_idx // per_col) == col_idx
        diag_start = (row_idx % per_col) * row_blk

        def diag_trace(mat_blk):
            square = lax.dynamic_slice_in_dim(mat_blk, diag_start, row_blk, axis=2)
            return jnp.where(on_diag, jnp.trace(square, axis1=1, axis2=2), 0.0)

        def left_operand(mat_blk):
            pieces = mat_blk.reshape(kpoints, row_blk, per_col, depth_size, sub_width)
            own_piece = lax.dynamic_index_in_dim(pieces, layer_idx, axis=3, keepdims=False)
            own_piece = own_piece.reshape(kpoints, row_blk, per_col * sub_width)
            return lax.all_gather(own_piece, 'col', axis=2, tiled=True)

        def right_operand(mat_blk):
            pieces = mat_blk.reshape(kpoints, depth_size, sub_width, col_blk)
            own_piece = lax.dynamic_index_in_dim(pieces, layer_idx, axis=1, keepdims=False)
            return lax.all_gather(own_piece, 'row', axis=1, tiled=True)

        def product(left_op, right_op):
            partial_prod = jnp.einsum('kab,kbc->kac', left_op, right_op, precision=highest, preferred_element_type=jnp.float32)
            return lax.psum(partial_prod, 'depth')

        occupied = occ_count.astype(jnp.float32)
        chem_pot = lax.psum(diag_trace(ham_blk), ('row', 'col')) / mat_order
        scale_fac = jnp.minimum(occupied / (spec_bounds[:, 1] - chem_pot), (mat_order - occupied) / (chem_pot - spec_bounds[:, 0]))
        diag_add = (scale_fac * chem_pot + occupied) / mat_order
        row_ids = lax.broadcasted_iota(jnp.int32, (row_blk, col_blk), 0) + row_idx * row_blk
        col_ids = lax.broadcasted_iota(jnp.int32, (row_blk, col_blk), 1) + col_idx * col_blk
        eye_blk = (row_ids == col_ids).astype(jnp.float32)
        density = diag_add[:, None, None] * eye_blk - (scale_fac / mat_order)[:, None, None] * ham_blk
        for step_idx in range(STEPS):
            dens_right = right_operand(density)
            dens_sq = product(left_operand(density), dens_right)
            dens_cube = product(left_operand(dens_sq), dens_right)
            local_traces = jnp.stack([diag_trace(density), jnp.sum(density * density, axis=(1, 2)), jnp.sum(dens_sq * density, axis=(1, 2))])
            traces = lax.psum(local_traces, ('row', 'col'))
            purify_coef = ((traces[1] - traces[2]) / (traces[0] - traces[1]))[:, None, None]
            density = ((1.0 - 2.0 * purify_coef) * density + (1.0 + purify_coef) * dens_sq - dens_cube) / (1.0 - purify_coef)
        energy = 2.0 * lax.psum(jnp.sum(density * ham_blk, axis=(1, 2)), ('row', 'col'))
        return density, energy

    mat_spec = P('spin', 'row', 'col')
    return jax.shard_map(local_purify, mesh=mesh, in_specs=(mat_spec, P('spin', None), P('spin')), out_specs=(mat_spec, P('spin')), check_vma=False)
```

profile of v0, /device:TPU:1, one launch (start us, length us, event | category | flops | bytes accessed | tf_op | source)
XLA Modules:
  0.0 7659.4 jit_solution(12566529597982078292)
XLA Ops:
  139.0 367.1 %all-gather.21.cloned.1.call-done = f32[16,1,768,768]{3,2,0,1:T(8,128)} async-done(((f32[16,1,384,768]{3,2,0,1:T(8,128)}), f32[16,1,768,768]{3,2,0,1:T(8,128)}) %all-gather.21.cloned.1.call-update) | async-done | bytes 37748752 | tf_op jit(solution)/shard_map/all_gather | solution.py:39
  506.1 56.6 all-gather.19.cloned.1.call-done
  562.7 97.4 %fusion.15 = f32[16,768,768]{2,1,0:T(8,128)} fusion(f32[16,1,768,768]{3,2,0,1:T(8,128)} %all-gather.21.cloned.1.call-done, f32[16,768,1,1,768]{4,1,0,3,2:T(8,128)} %all-gather.19.cloned.1.call-done), kind=kOutput, calls=%fused_computation.15 | convolution fusion | flops 86973087744 | bytes 113246208 | tf_op jit(solution)/shard_map/kab,kbc->kac/dot_general | solution.py:42
  660.2 822.5 %all-reduce.7.cloned.1.call-done = f32[16,768,768]{2,1,0:T(8,128)} async-done(((f32[16,768,768]{2,1,0:T(8,128)}), f32[16,768,768]{2,1,0:T(8,128)}) %all-reduce.7.cloned.1.call-update) | async-done | bytes 37748752 | tf_op jit(solution)/shard_map/psum | solution.py:43
  1557.0 56.9 all-gather.23.cloned.1.call-done
  1613.9 97.4 %fusion.12 = f32[16,768,768]{2,1,0:T(8,128)} fusion(f32[16,768,1,1,768]{4,1,0,3,2:T(8,128)} %all-gather.23.cloned.1.call-done, f32[16,1,768,768]{3,2,0,1:T(8,128)} %all-gather.21.cloned.1.call-done), kind=kOutput, calls=%fused_computation.12 | convolution fusion | flops 86973087744 | bytes 113246208 | tf_op jit(solution)/shard_map/kab,kbc->kac/dot_general | solution.py:42
  1744.1 789.8 %all-reduce.9.cloned.1.call-done = f32[16,768,768]{2,1,0:T(8,128)} async-done(((f32[16,768,768]{2,1,0:T(8,128)}), f32[16,768,768]{2,1,0:T(8,128)}) %all-reduce.9.cloned.1.call-update) | async-done | bytes 37748752 | tf_op jit(solution)/shard_map/psum | solution.py:43
  2533.9 49.8 subtract_divide_fusion.2
  2670.8 361.5 %all-gather.27.cloned.1.call-done = f32[16,1,768,768]{3,2,0,1:T(8,128)} async-done(((f32[16,1,384,768]{3,2,0,1:T(8,128)}), f32[16,1,768,768]{3,2,0,1:T(8,128)}) %all-gather.27.cloned.1.call-update) | async-done | bytes 37748752 | tf_op jit(solution)/shard_map/all_gather | solution.py:39
  3032.4 56.6 all-gather.25.cloned.1.call-done
  3089.0 97.3 %fusion.9 = f32[16,768,768]{2,1,0:T(8,128)} fusion(f32[16,1,768,768]{3,2,0,1:T(8,128)} %all-gather.27.cloned.1.call-done, f32[16,768,1,1,768]{4,1,0,3,2:T(8,128)} %all-gather.25.cloned.1.call-done), kind=kOutput, calls=%fused_computation.9 | convolution fusion | flops 86973087744 | bytes 113246208 | tf_op jit(solution)/shard_map/kab,kbc->kac/dot_general | solution.py:42
  3186.4 822.5 %all-reduce.11.cloned.1.call-done = f32[16,768,768]{2,1,0:T(8,128)} async-done(((f32[16,768,768]{2,1,0:T(8,128)}), f32[16,768,768]{2,1,0:T(8,128)}) %all-reduce.11.cloned.1.call-update) | async-done | bytes 37748752 | tf_op jit(solution)/shard_map/psum | solution.py:43
  4083.1 56.9 all-gather.29.cloned.1.call-done
  4140.1 97.3 %fusion.6 = f32[16,768,768]{2,1,0:T(8,128)} fusion(f32[16,768,1,1,768]{4,1,0,3,2:T(8,128)} %all-gather.29.cloned.1.call-done, f32[16,1,768,768]{3,2,0,1:T(8,128)} %all-gather.27.cloned.1.call-done), kind=kOutput, calls=%fused_computation.6 | convolution fusion | flops 86973087744 | bytes 113246208 | tf_op jit(solution)/shard_map/kab,kbc->kac/dot_general | solution.py:42
  4268.6 791.4 %all-reduce.13.cloned.1.call-done = f32[16,768,768]{2,1,0:T(8,128)} async-done(((f32[16,768,768]{2,1,0:T(8,128)}), f32[16,768,768]{2,1,0:T(8,128)}) %all-reduce.13.cloned.1.call-update) | async-done | bytes 37748752 | tf_op jit(solution)/shard_map/psum | solution.py:43
  5060.0 49.6 subtract_divide_fusion.1
  5196.5 361.7 %all-gather.33.cloned.1.call-done = f32[16,1,768,768]{3,2,0,1:T(8,128)} async-done(((f32[16,1,384,768]{3,2,0,1:T(8,128)}), f32[16,1,768,768]{3,2,0,1:T(8,128)}) %all-gather.33.cloned.1.call-update) | async-done | bytes 37748752 | tf_op jit(solution)/shard_map/all_gather | solution.py:39
  5558.2 56.5 all-gather.31.cloned.1.call-done
  5614.7 97.3 %fusion.3 = f32[16,768,768]{2,1,0:T(8,128)} fusion(f32[16,1,768,768]{3,2,0,1:T(8,128)} %all-gather.33.cloned.1.call-done, f32[16,768,1,1,768]{4,1,0,3,2:T(8,128)} %all-gather.31.cloned.1.call-done), kind=kOutput, calls=%fused_computation.3 | convolution fusion | flops 86973087744 | bytes 113246208 | tf_op jit(solution)/shard_map/kab,kbc->kac/dot_general | solution.py:42
  5712.1 822.5 %all-reduce.15.cloned.1.call-done = f32[16,768,768]{2,1,0:T(8,128)} async-done(((f32[16,768,768]{2,1,0:T(8,128)}), f32[16,768,768]{2,1,0:T(8,128)}) %all-reduce.15.cloned.1.call-update) | async-done | bytes 37748752 | tf_op jit(solution)/shard_map/psum | solution.py:43
  6608.9 56.9 all-gather.35.cloned.1.call-done
  6665.8 97.3 %fusion = f32[16,768,768]{2,1,0:T(8,128)} fusion(f32[16,768,1,1,768]{4,1,0,3,2:T(8,128)} %all-gather.35.cloned.1.call-done, f32[16,1,768,768]{3,2,0,1:T(8,128)} %all-gather.33.cloned.1.call-done), kind=kOutput, calls=%fused_computation | convolution fusion | flops 86973087744 | bytes 113246208 | tf_op jit(solution)/shard_map/kab,kbc->kac/dot_general | solution.py:42
  6794.3 791.4 %all-reduce.17.cloned.1.call-done = f32[16,768,768]{2,1,0:T(8,128)} async-done(((f32[16,768,768]{2,1,0:T(8,128)}), f32[16,768,768]{2,1,0:T(8,128)}) %all-reduce.17.cloned.1.call-update) | async-done | bytes 37748752 | tf_op jit(solution)/shard_map/psum | solution.py:43
  7585.7 60.5 multiply_reduce_fusion
  (104 shorter events, 630.0 us)
Async XLA Ops:
  7.2 21.5 copy-start.11
  7.2 21.5 copy-start.10
  7.2 498.9 %all-gather.21.cloned.1.call-start = ((), (), s32[]{:S(2)}) async-start(), calls=%async_computation.7 | async-start | bytes 56623104 | tf_op jit(solution)/shard_map/all_gather | solution.py:39
  7.4 21.3 copy-start.2
  28.7 29.6 copy-start.6
  28.7 29.5 copy-start.8
  29.0 29.3 copy-start
  70.9 491.9 %all-gather.19.cloned.1.call-start = ((), (), s32[]{:S(2)}) async-start(), calls=%async_computation.6 | async-start | bytes 56623104 | tf_op jit(solution)/shard_map/all_gather | solution.py:34
  139.0 1343.7 %all-reduce.7.cloned.1.call-start = ((), (), s32[]{:S(2)}) async-start(), calls=%async_computation | async-start | bytes 75497472 | tf_op jit(solution)/shard_map/psum | solution.py:43
  660.1 953.8 %all-gather.23.cloned.1.call-start = ((), (), s32[]{:S(2)}) async-start(), calls=%async_computation.8 | async-start | bytes 56623104 | tf_op jit(solution)/shard_map/all_gather | solution.py:34
  1556.8 977.1 %all-reduce.9.cloned.1.call-start = ((), (), s32[]{:S(2)}) async-start(), calls=%async_computation.1 | async-start | bytes 75497472 | tf_op jit(solution)/shard_map/psum | solution.py:43
  1711.3 1.8 copy-start.3
  1711.3 1.8 copy-start.7
  1711.3 1.8 copy-start.9
  1711.4 1321.0 %all-gather.27.cloned.1.call-start = ((), (), s32[]{:S(2)}) async-start(), calls=%async_computation.10 | async-start | bytes 56623104 | tf_op jit(solution)/shard_map/all_gather | solution.py:39
  2596.3 492.7 %all-gather.25.cloned.1.call-start = ((), (), s32[]{:S(2)}) async-start(), calls=%async_computation.9 | async-start | bytes 56623104 | tf_op jit(solution)/shard_map/all_gather | solution.py:34
  2670.4 1338.5 %all-reduce.11.cloned.1.call-start = ((), (), s32[]{:S(2)}) async-start(), calls=%async_computation.2 | async-start | bytes 75497472 | tf_op jit(solution)/shard_map/psum | solution.py:43
  3186.4 953.7 %all-gather.29.cloned.1.call-start = ((), (), s32[]{:S(2)}) async-start(), calls=%async_computation.11 | async-start | bytes 56623104 | tf_op jit(solution)/shard_map/all_gather | solution.py:34
  4082.9 977.1 %all-reduce.13.cloned.1.call-start = ((), (), s32[]{:S(2)}) async-start(), calls=%async_computation.3 | async-start | bytes 75497472 | tf_op jit(solution)/shard_map/psum | solution.py:43
  4237.4 1320.8 %all-gather.33.cloned.1.call-start = ((), (), s32[]{:S(2)}) async-start(), calls=%async_computation.13 | async-start | bytes 56623104 | tf_op jit(solution)/shard_map/all_gather | solution.py:39
  5122.2 492.5 %all-gather.31.cloned.1.call-start = ((), (), s32[]{:S(2)}) async-start(), calls=%async_computation.12 | async-start | bytes 56623104 | tf_op jit(solution)/shard_map/all_gather | solution.py:34
  5196.2 1338.4 %all-reduce.15.cloned.1.call-start = ((), (), s32[]{:S(2)}) async-start(), calls=%async_computation.4 | async-start | bytes 75497472 | tf_op jit(solution)/shard_map/psum | solution.py:43
  5712.1 953.7 %all-gather.35.cloned.1.call-start = ((), (), s32[]{:S(2)}) async-start(), calls=%async_computation.14 | async-start | bytes 56623104 | tf_op jit(solution)/shard_map/all_gather | solution.py:34
  6608.6 977.1 %all-reduce.17.cloned.1.call-start = ((), (), s32[]{:S(2)}) async-start(), calls=%async_computation.5 | async-start | bytes 75497472 | tf_op jit(solution)/shard_map/psum | solution.py:43
  (3 other events, 3.8 us)
Sparse Core Ops, SparseCore 0:
  71.0 435.0 all-gather.20
  507.6 55.0 all-gather.18
  660.2 822.3 all-reduce.6
  1556.9 56.9 all-gather.22
  1711.5 822.3 all-reduce.8
  2596.4 435.8 all-gather.26
  3033.9 55.0 all-gather.24
  3186.5 822.3 all-reduce.10
  4083.0 56.9 all-gather.28
  4237.6 822.3 all-reduce.12
  5122.3 435.8 all-gather.32
  5559.6 55.0 all-gather.30
  5712.2 822.3 all-reduce.14
  6608.8 56.9 all-gather.34
  6763.3 822.3 all-reduce.16
where the time goes:
time: 7670 us; the launch traced here: 7660 us
  waiting for transfers between devices  6270 us (82%)
  matrix products  584 us (8%)
  local copies, waits for them, and re-layouts  479 us (6%)
  other arithmetic  279 us (4%)
    psum x6, waiting for transfers between devices, product(): return lax.psum(partial_prod, 'depth')  4840 us
    all_gather x3, waiting for transfers between devices, right_operand(): return lax.all_gather(own_piece, 'row', axis=1, tiled=True)  1090 us
    dot_general x6, matrix products, product(): jnp.einsum('kab,kbc->kac', left_op, right_op, precision=highest, preferre...  584 us
    all_gather x6, waiting for transfers between devices, left_operand(): return lax.all_gather(own_piece, 'col', axis=2, tiled=True)  340 us
    reshape x5, local copies, waits for them, and re-layouts, left_operand(): pieces = mat_blk.reshape(kpoints, row_blk, per_col, depth_size, sub_width)  225 us
  transfers between devices with their start and end apart: 15, of which 15 were waited for; matrix products, arithmetic and copies ran while one was open for 4% of the time, Pallas kernels for 0%

commit v1 on v0

v1 whole, which is shorter than its diff:
```python
import functools

import jax
import jax.numpy as jnp
from jax import lax
from jax.experimental import pallas as pl
from jax.experimental.pallas import tpu as pltpu
from jax.sharding import PartitionSpec as P

STEPS = 3
G = 3
NB = 2 * G
UPPER = NB * (NB + 1) // 2
F32 = jnp.float32
BF16 = jnp.bfloat16
PASSES = ((0, 2), (2, 0), (1, 1), (0, 1), (1, 0), (0, 0))
MESH = pl.DeviceIdType.MESH


def slot_of(row, col):
    return row * (2 * NB - 1 - row) // 2 + col


def slot3_of(row, col):
    return row * (2 * G - 1 - row) // 2 + col


def upper_tile(row, step):
    wrap = (row + step) // NB
    other = row + step - NB * wrap
    return row * (1 - wrap) + other * wrap, other * (1 - wrap) + row * wrap


def limbs(val):
    high = val.astype(BF16)
    rest = val - high.astype(F32)
    mid = rest.astype(BF16)
    low = (rest - mid.astype(F32)).astype(BF16)
    return high, mid, low


def put(ref, row, col, val, diag):
    for piece, part in enumerate(limbs(val)):
        ref[piece, row, col] = part
    if not diag:
        for piece, part in enumerate(limbs(val.T)):
            ref[piece, col, row] = part


def get(ref, row, col):
    low = ref[1, row, col].astype(F32) + ref[2, row, col].astype(F32)
    return ref[0, row, col].astype(F32) + low


def chain(left, right, row, col, passes):
    acc = None
    for k in range(NB):
        for p, q in passes:
            part = jnp.dot(left[p, row, k], right[q, k, col], preferred_element_type=F32)
            acc = part if acc is None else acc + part
    return acc


def fold(val):
    size = val.shape[0]
    return jnp.sum(val.reshape(size // 8, 8, val.shape[1]), axis=0)


def total(val):
    return jnp.sum(jnp.sum(val, axis=0, keepdims=True), axis=1, keepdims=True)


def flip(bit, by):
    return bit + by - 2 * bit * by


def main_kernel(
    bounds, occ, ham, land, ener,
    buf_a, buf_b, buf_c, stage, sums, e_vec,
    so_sem, r_sem, in_send, land_sem, out_send, e_sem, e_send,
):
    tile = stage.shape[2]
    order = NB * tile
    y, x, c = lax.axis_index('depth'), lax.axis_index('row'), lax.axis_index('col')
    own = y * 4 + x * 2 + c
    differ = flip(x, c)

    def device(dy, dx, cd):
        return {'depth': dy, 'row': dx, 'col': cd}

    barrier = pltpu.get_barrier_semaphore()
    for k in range(1, 8):
        pl.semaphore_signal(
            barrier, inc=1,
            device_id=device(flip(y, k // 4), flip(x, (k // 2) % 2), flip(c, k % 2)),
            device_id_type=MESH,
        )
    pl.semaphore_wait(barrier, 7)

    def h_tile(mat, i, j):
        return ham.at[mat, pl.ds(i * tile, tile), pl.ds(j * tile, tile)]

    diag_tiles = [(i, j) for i in range(G) for j in range(i, G)]
    full_tiles = [(i, j) for i in range(G) for j in range(G)]

    def send_in(rnd, carry):
        other = own + 1 - 2 * c

        @pl.when(differ == 0)
        def _():
            for i, j in diag_tiles:
                for cd in range(2):
                    mat = rnd * 8 + y * 4 + (1 - x) * 2 + cd
                    pltpu.make_async_remote_copy(
                        h_tile(mat, i, j), stage.at[rnd, slot_of(G + i, G + j)],
                        in_send, r_sem.at[rnd],
                        device_id=device(y, 1 - x, cd), device_id_type=MESH,
                    ).start()
            for i, j in diag_tiles:
                pltpu.make_async_copy(
                    h_tile(rnd * 8 + own, i, j), stage.at[rnd, slot_of(i, j)], so_sem.at[rnd]
                ).start()
                pltpu.make_async_remote_copy(
                    h_tile(rnd * 8 + other, i, j), stage.at[rnd, slot_of(i, j)],
                    in_send, so_sem.at[rnd],
                    device_id=device(y, x, 1 - c), device_id_type=MESH,
                ).start()

        @pl.when(differ == 1)
        def _():
            for i, j in full_tiles:
                pltpu.make_async_copy(
                    h_tile(rnd * 8 + own, i, j), stage.at[rnd, slot_of(i, G + j)], so_sem.at[rnd]
                ).start()
                pltpu.make_async_remote_copy(
                    h_tile(rnd * 8 + other, i, j), stage.at[rnd, slot_of(i, G + j)],
                    in_send, so_sem.at[rnd],
                    device_id=device(y, x, 1 - c), device_id_type=MESH,
                ).start()

        return carry

    lax.fori_loop(0, 2, send_in, 0)

    def wait_for(ref, sem):
        pltpu.make_async_copy(ref, ref, sem).wait()

    rows = lax.broadcasted_iota(jnp.int32, (tile, tile), 0)
    cols = lax.broadcasted_iota(jnp.int32, (tile, tile), 1)
    eye = jnp.where(rows == cols, 1.0, 0.0).astype(F32)

    def send_out(rnd, row, col):
        mat = rnd * 8 + own
        src = stage.at[rnd, slot_of(row, col)]
        k_row, k_col = row // G, col // G

        def start(dy, xd, cd, dst, may_be_self):
            def remote():
                pltpu.make_async_remote_copy(
                    src, dst, out_send, land_sem,
                    device_id=device(flip(y, dy), xd, cd), device_id_type=MESH,
                ).start()

            if may_be_self:
                pl.when(cd == c)(lambda: pltpu.make_async_copy(src, dst, land_sem).start())
                pl.when(cd != c)(remote)
            else:
                remote()

        @pl.when(k_col == 1)
        def _():
            place = k_row * slot3_of(row - G, col - G) + (1 - k_row) * (row * G + col - G)
            dst = land.at[mat * (9 - 3 * k_row) + place]
            cd = (1 - x) * k_row + x * (1 - k_row)
            start(0, 1 - x, cd, dst, False)
            start(1, 1 - x, cd, dst, False)

        @pl.when(k_row == 0)
        def _():
            place = (1 - k_col) * slot3_of(row, col) + k_col * (row * G + col - G)
            dst = land.at[mat * (6 + 3 * k_col) + place]
            cd = x * (1 - k_col) + (1 - x) * k_col
            start(1, x, cd, dst, False)
            start(0, x, cd, dst, True)

    def tiles_of(turn):
        out = []
        for half in range(2):
            row = turn * 2 + half
            for step in range(3):
                out.append((*upper_tile(row, step), step == 0))
        out.append((turn, turn + 3, False))
        return out

    def square(src):
        def turn(v, carry):
            for row, col, diag in tiles_of(v):
                if diag:
                    cross = chain(src, src, row, col, ((0, 2), (0, 1)))
                    val = chain(src, src, row, col, ((1, 1), (0, 0)))
                    val = val + (cross + cross.T)
                else:
                    val = chain(src, src, row, col, PASSES)
                put(buf_b, row, col, val, diag)
                sums[2] += fold(val * get(src, row, col)) * (1.0 if diag else 2.0)
            return carry

        sums[2] = jnp.zeros_like(sums[2])
        lax.fori_loop(0, 3, turn, 0)

    def coefs():
        t1, t2, t3 = total(sums[0]), total(sums[1]), total(sums[2])
        coef = (t2 - t3) / (t1 - t2)
        inv = 1.0 / (1.0 - coef)
        return (1.0 - 2.0 * coef) * inv, (1.0 + coef) * inv, inv

    def count(val, diag):
        if diag:
            sums[0] += fold(val * eye)
        sums[1] += fold(val * val) * (1.0 if diag else 2.0)

    def combine(src, row, col, co):
        acc = chain(buf_b, src, row, col, PASSES)
        return co[0] * get(src, row, col) + co[1] * get(buf_b, row, col) - co[2] * acc

    def cube(src, dst):
        co = coefs()
        sums[0:2] = jnp.zeros_like(sums[0:2])

        def turn(v, carry):
            for row, col, diag in tiles_of(v):
                val = combine(src, row, col, co)
                put(dst, row, col, val, diag)
                count(val, diag)
            return carry

        lax.fori_loop(0, 3, turn, 0)

    def cube_last(src, rnd):
        co = coefs()
        sums[0] = jnp.zeros_like(sums[0])

        def unit(v, step):
            last = v // NB
            row, col = upper_tile(v * (1 - last), step)
            return row * (1 - last) + step * last, col * (1 - last) + (step + 3) * last

        def turn(v, carry):
            @pl.when(v > 0)
            def _():
                for step in range(3):
                    send_out(rnd, *unit(v - 1, step))

            for step in range(3):
                row, col = unit(v, step)
                val = combine(src, row, col, co)
                slot = slot_of(row, col)
                weight = 2.0 if step else 1.0 + (v // NB).astype(F32)
                sums[0] += fold(val * stage[rnd, slot]) * weight
                stage[rnd, slot] = val
            return carry

        lax.fori_loop(0, 7, turn, 0)
        for step in range(3):
            send_out(rnd, *unit(6, step))

    def one_matrix(rnd, carry):
        mat = rnd * 8 + own
        wait_for(stage.at[rnd, pl.ds(0, 15)], so_sem.at[rnd])
        wait_for(stage.at[rnd, pl.ds(15, 6)], r_sem.at[rnd])
        diag_sum = fold(stage[rnd, slot_of(0, 0)] * eye)
        for i in range(1, NB):
            diag_sum += fold(stage[rnd, slot_of(i, i)] * eye)
        mean = total(diag_sum) / order
        filled = occ[mat].astype(F32)
        scale = jnp.minimum(
            filled / (bounds[mat, 1] - mean), (order - filled) / (mean - bounds[mat, 0])
        )
        on_diag = (scale * mean + filled) / order
        slope = scale / order
        sums[0:2] = jnp.zeros_like(sums[0:2])

        def first(v, c_):
            for row, col, diag in tiles_of(v):
                val = stage[rnd, slot_of(row, col)] * -slope
                if diag:
                    val = val + on_diag * eye
                put(buf_a, row, col, val, diag)
                count(val, diag)
            return c_

        lax.fori_loop(0, 3, first, 0)

        def step(s, c_):
            pl.when(s != 1)(lambda: square(buf_a))
            pl.when(s == 1)(lambda: square(buf_c))
            pl.when(s == 0)(lambda: cube(buf_a, buf_c))
            pl.when(s == 1)(lambda: cube(buf_c, buf_a))
            pl.when(s == 2)(lambda: cube_last(buf_a, rnd))
            return c_

        lax.fori_loop(0, STEPS, step, 0)
        e_vec[rnd] = jnp.broadcast_to(2.0 * total(sums[0]), e_vec.shape[1:])
        for k in range(1, 8):
            pltpu.make_async_remote_copy(
                e_vec.at[rnd], ener.at[mat], e_send, e_sem,
                device_id=device(flip(y, k // 4), flip(x, (k // 2) % 2), flip(c, k % 2)),
                device_id_type=MESH,
            ).start()
        pltpu.make_async_copy(e_vec.at[rnd], ener.at[mat], e_sem).start()
        return carry

    lax.fori_loop(0, 2, one_matrix, 0)

    wait_for(ener.at[pl.ds(0, 14)], e_send)
    wait_for(ener, e_sem)

    @pl.when(differ == 0)
    def _():
        wait_for(land.at[pl.ds(0, 36)], in_send)
        wait_for(land.at[pl.ds(0, 108)], out_send)
        wait_for(land.at[pl.ds(0, 96)], land_sem)

    @pl.when(differ == 1)
    def _():
        wait_for(land.at[pl.ds(0, 18)], in_send)
        wait_for(land.at[pl.ds(0, 102)], out_send)
        wait_for(land, land_sem)


def unpack_kernel(where, in0, in1, in2, out):
    tile = in0.shape[2]
    mat = pl.program_id(0)
    x, differ = where[0], where[1]
    turned = flip((mat // 2) % 2, x)

    def at(i, j):
        return (0, pl.ds(i * tile, tile), pl.ds(j * tile, tile))

    @pl.when(differ == 0)
    def _():
        packed = [in0[0, 0], in0[0, 1], in0[0, 2], in1[0, 0], in1[0, 1], in1[0, 2]]
        for i in range(G):
            for j in range(i, G):
                val = packed[slot3_of(i, j)]
                out[at(i, j)] = val
                if i != j:
                    out[at(j, i)] = val.T

    @pl.when(differ * (1 - turned) == 1)
    def _():
        for i, ref in enumerate((in0, in1, in2)):
            for j in range(G):
                out[at(i, j)] = ref[0, j]

    @pl.when(differ * turned == 1)
    def _():
        for i, ref in enumerate((in0, in1, in2)):
            for j in range(G):
                out[at(j, i)] = ref[0, j].T


def solution(mesh):
    def local_purify(ham, bounds, occ):
        mats, blk, _ = ham.shape
        tile = blk // G
        x, c = lax.axis_index('row'), lax.axis_index('col')
        any_spec = pl.BlockSpec(memory_space=pltpu.HBM)
        smem = pl.BlockSpec(memory_space=pltpu.SMEM)
        limb = pltpu.VMEM((3, NB, NB, tile, tile), BF16)
        flops = 2 * 6 * 21 * 36 * 2 * tile**3
        land, ener = pl.pallas_call(
            main_kernel,
            out_shape=(
                jax.ShapeDtypeStruct((mats * G * G, tile, tile), F32),
                jax.ShapeDtypeStruct((mats, 8, 128), F32),
            ),
            in_specs=[smem, smem, any_spec],
            out_specs=(any_spec, any_spec),
            scratch_shapes=[
                limb, limb, limb,
                pltpu.VMEM((2, UPPER, tile, tile), F32),
                pltpu.VMEM((3, 8, tile), F32),
                pltpu.VMEM((2, 8, 128), F32),
                pltpu.SemaphoreType.DMA((2,)),
                pltpu.SemaphoreType.DMA((2,)),
                pltpu.SemaphoreType.DMA,
                pltpu.SemaphoreType.DMA,
                pltpu.SemaphoreType.DMA,
                pltpu.SemaphoreType.DMA,
                pltpu.SemaphoreType.DMA,
            ],
            compiler_params=pltpu.CompilerParams(
                collective_id=0, has_side_effects=True, vmem_limit_bytes=67043328
            ),
            cost_estimate=pl.CostEstimate(flops=flops, bytes_accessed=120 * 2**20, transcendentals=0),
            name='purify',
        )(bounds, occ, ham)

        where = jnp.stack([x, x + c - 2 * x * c]).astype(jnp.int32)
        quads = land.reshape(mats * G, G, tile, tile)

        def part(k):
            def index(m, ref):
                off = ref[1]
                last = 0 if k == 2 else 2 * m + k
                return off * (3 * m + k) + (1 - off) * last, 0, 0, 0

            return pl.BlockSpec((1, G, tile, tile), index)

        density = pl.pallas_call(
            unpack_kernel,
            out_shape=jax.ShapeDtypeStruct(ham.shape, F32),
            grid_spec=pltpu.PrefetchScalarGridSpec(
                num_scalar_prefetch=1,
                grid=(mats,),
                in_specs=[part(0), part(1), part(2)],
                out_specs=pl.BlockSpec((1, blk, blk), lambda m, ref: (m, 0, 0)),
            ),
            compiler_params=pltpu.CompilerParams(vmem_limit_bytes=40 * 2**20),
            cost_estimate=pl.CostEstimate(flops=10**6, bytes_accessed=75 * 2**20, transcendentals=0),
            name='unpack',
        )(where, quads, quads, quads)
        return density, ener[:, 0, 0]

    mat_spec = P('spin', 'row', 'col')
    return jax.shard_map(
        local_purify, mesh=mesh,
        in_specs=(mat_spec, P('spin', None), P('spin')),
        out_specs=(mat_spec, P('spin')), check_vma=False,
    )
```

time: 7670 us -> 559 us (0.07)
  waiting for transfers between devices: 6270 us -> 0 us
  matrix products: 584 us -> 0 us
  Pallas kernels: 0 us -> 553 us
  local copies, waits for them, and re-layouts: 479 us -> 3.53 us
  other arithmetic: 279 us -> 0.62 us
    psum x6 -> x0, waiting for transfers between devices: 4840 us -> none  [product(): return lax.psum(partial_prod, 'depth')]
    all_gather x9 -> x0, waiting for transfers between devices: 1430 us -> none  [the longest x3 1090 us: right_operand(): return lax.all_gather(own_piece, 'row', axis=1, tiled=True)]
    dot_general x6 -> x0, matrix products: 584 us -> none  [product(): jnp.einsum('kab,kbc->kac', left_op, right_op, precision=highest, preferre...]
    pallas_call x0 -> x2, Pallas kernels: none -> 553 us  [the longest x1 522 us: local_purify(): pl.pallas_call(main_kernel, out_shape=(jax.ShapeDtypeStruct((mats * G * G...]
    reshape x5 -> x0, local copies, waits for them, and re-layouts: 225 us -> none  [left_operand(): pieces = mat_blk.reshape(kpoints, row_blk, per_col, depth_size, sub_width)]
    reduce_sum x5 -> x0, other arithmetic: 149 us -> none  [the longest x4 88.9 us: diag_trace(): return jnp.where(on_diag, jnp.trace(square, axis1=1, axis2=2), 0.0)]
    dynamic_slice x6 -> x0, local copies, waits for them, and re-layouts: 122 us -> none  [left_operand(): lax.dynamic_index_in_dim(pieces, layer_idx, axis=3, keepdims=False)]
    div x4 -> x0, other arithmetic: 99.4 us -> none  [the longest x2 99.4 us: local_purify(): ((1.0 - 2.0 * purify_coef) * density + (1.0 + purify_coef) * dens_sq - de...]
  transfers between devices with their start and end apart: 15 -> 0, of which waited for: 15 -> 0; matrix products, arithmetic and copies ran while one was open for 4% -> 0% of each run, Pallas kernels for 0% -> 0%
where the time goes in v1:
time: 559 us; the launch traced here: 558 us
  Pallas kernels  553 us (99%)
    pallas_call x1, Pallas kernels, local_purify(): pl.pallas_call(main_kernel, out_shape=(jax.ShapeDtypeStruct((mats * G * G...  522 us
    pallas_call x1, Pallas kernels, local_purify(): pl.pallas_call(unpack_kernel, out_shape=jax.ShapeDtypeStruct(ham.shape, F...  31.5 us

profile of v1, /device:TPU:1, one launch (start us, length us, event | category | flops | bytes accessed | tf_op | source)
XLA Modules:
  0.0 558.1 jit_solution(2221620607874705553)
XLA Ops:
  0.6 0.6 pad_add_fusion.where
  1.3 1.4 copy.6.bounds
  2.6 521.8 %purify.1 = (f32[144,256,256]{2,1,0:T(8,128)}, f32[16,8,128]{2,1,0:T(8,128)}) custom-call(f32[16,2]{1,0:T(8,128)} %copy.6.bounds, s32[16]{0:T(128)} %occ.1, f32[16,768,768]{2,1,0:T(8,128)} %ham.1), custom_call_target="tpu_custom_call" | custom-call | flops 304405807104 | bytes 125829120 | tf_op jit(solution)/shard_map/purify/pallas_call | solution.py:372
  524.4 0.0 copy-start
  524.4 0.6 copy-done
  525.0 31.5 %unpack.1 = f32[16,768,768]{2,1,0:T(8,128)} custom-call(s32[2]{0:T(128)S(1)} %copy-done, f32[48,3,256,256]{3,2,1,0:T(8,128)} %bitcast.3, f32[48,3,256,256]{3,2,1,0:T(8,128)} %bitcast.4, f32[48,3,256,256]{3,2,1,0:T(8,128)} %bitcast.5), custom_call_target="tpu_custom_call" | custom-call | flops 1000000 | bytes 78643200 | tf_op jit(solution)/shard_map/unpack/pallas_call | solution.py:411
  556.5 1.6 slice_reduce_fusion
Async XLA Ops:
  524.4 0.6 copy-start

commit v2 on v1

--- a/solution.py
+++ b/solution.py
@@ -11,6 +11,7 @@
 G = 3
 NB = 2 * G
 UPPER = NB * (NB + 1) // 2
+UPPER3 = G * (G + 1) // 2
 F32 = jnp.float32
 BF16 = jnp.bfloat16
 PASSES = ((0, 2), (2, 0), (1, 1), (0, 1), (1, 0), (0, 0))
@@ -77,7 +78,7 @@
 def main_kernel(
     bounds, occ, ham, land, ener,
     buf_a, buf_b, buf_c, stage, sums, e_vec,
-    so_sem, r_sem, in_send, land_sem, out_send, e_sem, e_send,
+    so_sem, r_sem, in_send, land_sem, relay_sem, out_send, e_sem, e_send,
 ):
     tile = stage.shape[2]
     order = NB * tile
@@ -108,8 +109,8 @@
 
         @pl.when(differ == 0)
         def _():
-            for i, j in diag_tiles:
-                for cd in range(2):
+            for cd in range(2):
+                for i, j in diag_tiles:
                     mat = rnd * 8 + y * 4 + (1 - x) * 2 + cd
                     pltpu.make_async_remote_copy(
                         h_tile(mat, i, j), stage.at[rnd, slot_of(G + i, G + j)],
@@ -154,34 +155,52 @@
         src = stage.at[rnd, slot_of(row, col)]
         k_row, k_col = row // G, col // G
 
-        def start(dy, xd, cd, dst, may_be_self):
-            def remote():
+        def start(dy, xd, cd, dst, sem):
+            pltpu.make_async_remote_copy(
+                src, dst, out_send, sem,
+                device_id=device(flip(y, dy), xd, cd), device_id_type=MESH,
+            ).start()
+
+        @pl.when(k_row + k_col == 1)
+        def _():
+            place = row * G + col - G
+            dst = land.at[mat * 9 + place]
+            start(1, x, 1 - x, dst, relay_sem.at[rnd, c, place])
+            start(0, 1 - x, x, dst, land_sem)
+            pl.when(differ == 1)(lambda: pltpu.make_async_copy(src, dst, land_sem).start())
+            pl.when(differ == 0)(lambda: start(0, x, 1 - x, dst, land_sem))
+
+        @pl.when(k_row == 1)
+        def _():
+            place = slot3_of(row - G, col - G)
+            start(0, 1 - x, 1 - x, land.at[mat * 6 + place], relay_sem.at[rnd, c, place])
+
+        @pl.when(k_col == 0)
+        def _():
+            dst = land.at[mat * 6 + slot3_of(row, col)]
+            start(1, x, x, dst, land_sem)
+            pl.when(differ == 0)(lambda: pltpu.make_async_copy(src, dst, land_sem).start())
+            pl.when(differ == 1)(lambda: start(0, x, x, dst, land_sem))
+
+    def relay(rnd, place):
+        def pass_on(first_owner, per, dev):
+            for cd in range(2):
+                tile_ref = land.at[(rnd * 8 + first_owner + cd) * per + place]
+                wait_for(tile_ref, relay_sem.at[rnd, cd, place])
                 pltpu.make_async_remote_copy(
-                    src, dst, out_send, land_sem,
-                    device_id=device(flip(y, dy), xd, cd), device_id_type=MESH,
+                    tile_ref, tile_ref, out_send, land_sem, device_id=dev, device_id_type=MESH
                 ).start()
 
-            if may_be_self:
-                pl.when(cd == c)(lambda: pltpu.make_async_copy(src, dst, land_sem).start())
-                pl.when(cd != c)(remote)
-            else:
-                remote()
-
-        @pl.when(k_col == 1)
-        def _():
-            place = k_row * slot3_of(row - G, col - G) + (1 - k_row) * (row * G + col - G)
-            dst = land.at[mat * (9 - 3 * k_row) + place]
-            cd = (1 - x) * k_row + x * (1 - k_row)
-            start(0, 1 - x, cd, dst, False)
-            start(1, 1 - x, cd, dst, False)
-
-        @pl.when(k_row == 0)
-        def _():
-            place = (1 - k_col) * slot3_of(row, col) + k_col * (row * G + col - G)
-            dst = land.at[mat * (6 + 3 * k_col) + place]
-            cd = x * (1 - k_col) + (1 - x) * k_col
-            start(1, x, cd, dst, False)
-            start(0, x, cd, dst, True)
+        @pl.when(differ == 1)
+        def _():
+            pass_on((1 - y) * 4 + x * 2, 9, device(y, 1 - x, x))
+
+        @pl.when((differ == 0) & (place < UPPER3))
+        def _():
+            pass_on(y * 4 + (1 - x) * 2, 6, device(1 - y, x, x))
+
+    def relay_early(rnd, turn):
+        pl.when((rnd == 1) & (turn >= 3) & (turn < 3 + G * G))(lambda: relay(0, turn - 3))
 
     def tiles_of(turn):
         out = []
@@ -192,8 +211,9 @@
         out.append((turn, turn + 3, False))
         return out
 
-    def square(src):
+    def square(src, rnd, before):
         def turn(v, carry):
+            relay_early(rnd, before + v)
             for row, col, diag in tiles_of(v):
                 if diag:
                     cross = chain(src, src, row, col, ((0, 2), (0, 1)))
@@ -223,11 +243,12 @@
         acc = chain(buf_b, src, row, col, PASSES)
         return co[0] * get(src, row, col) + co[1] * get(buf_b, row, col) - co[2] * acc
 
-    def cube(src, dst):
+    def cube(src, dst, rnd, before):
         co = coefs()
         sums[0:2] = jnp.zeros_like(sums[0:2])
 
         def turn(v, carry):
+            relay_early(rnd, before + v)
             for row, col, diag in tiles_of(v):
                 val = combine(src, row, col, co)
                 put(dst, row, col, val, diag)
@@ -241,9 +262,12 @@
         sums[0] = jnp.zeros_like(sums[0])
 
         def unit(v, step):
-            last = v // NB
-            row, col = upper_tile(v * (1 - last), step)
-            return row * (1 - last) + step * last, col * (1 - last) + (step + 3) * last
+            late = (v + 3) // 6
+            half = (v - 3) % 2
+            base = G * (1 - (v - 3) // 2)
+            row = base + half * (1 + step // 2)
+            col = base + (1 - half) * step + half * (1 + (step + 1) // 2)
+            return row * late + v * (1 - late), col * late + (G + step) * (1 - late)
 
         def turn(v, carry):
             @pl.when(v > 0)
@@ -255,7 +279,7 @@
                 row, col = unit(v, step)
                 val = combine(src, row, col, co)
                 slot = slot_of(row, col)
-                weight = 2.0 if step else 1.0 + (v // NB).astype(F32)
+                weight = jnp.where(row == col, 1.0, 2.0)
                 sums[0] += fold(val * stage[rnd, slot]) * weight
                 stage[rnd, slot] = val
             return carry
@@ -274,7 +298,7 @@
         mean = total(diag_sum) / order
         filled = occ[mat].astype(F32)
         scale = jnp.minimum(
-            filled / (bounds[mat, 1] - mean), (order - filled) / (mean - bounds[mat, 0])
+            filled / (bounds[1, mat] - mean), (order - filled) / (mean - bounds[0, mat])
         )
         on_diag = (scale * mean + filled) / order
         slope = scale / order
@@ -292,10 +316,10 @@
         lax.fori_loop(0, 3, first, 0)
 
         def step(s, c_):
-            pl.when(s != 1)(lambda: square(buf_a))
-            pl.when(s == 1)(lambda: square(buf_c))
-            pl.when(s == 0)(lambda: cube(buf_a, buf_c))
-            pl.when(s == 1)(lambda: cube(buf_c, buf_a))
+            pl.when(s != 1)(lambda: square(buf_a, rnd, 6 * s))
+            pl.when(s == 1)(lambda: square(buf_c, rnd, 6))
+            pl.when(s == 0)(lambda: cube(buf_a, buf_c, rnd, 3))
+            pl.when(s == 1)(lambda: cube(buf_c, buf_a, rnd, 9))
             pl.when(s == 2)(lambda: cube_last(buf_a, rnd))
             return c_
 
@@ -312,52 +336,59 @@
 
     lax.fori_loop(0, 2, one_matrix, 0)
 
+    for place in range(G * G):
+        relay(1, place)
     wait_for(ener.at[pl.ds(0, 14)], e_send)
     wait_for(ener, e_sem)
 
     @pl.when(differ == 0)
     def _():
         wait_for(land.at[pl.ds(0, 36)], in_send)
-        wait_for(land.at[pl.ds(0, 108)], out_send)
-        wait_for(land.at[pl.ds(0, 96)], land_sem)
+        wait_for(land.at[pl.ds(0, 102)], out_send)
+        wait_for(land.at[pl.ds(0, 72)], land_sem)
 
     @pl.when(differ == 1)
     def _():
         wait_for(land.at[pl.ds(0, 18)], in_send)
-        wait_for(land.at[pl.ds(0, 102)], out_send)
-        wait_for(land, land_sem)
+        wait_for(land.at[pl.ds(0, 108)], out_send)
+        wait_for(land.at[pl.ds(0, 108)], land_sem)
+
+
+PER = 2
 
 
 def unpack_kernel(where, in0, in1, in2, out):
     tile = in0.shape[2]
-    mat = pl.program_id(0)
     x, differ = where[0], where[1]
-    turned = flip((mat // 2) % 2, x)
-
-    def at(i, j):
-        return (0, pl.ds(i * tile, tile), pl.ds(j * tile, tile))
-
-    @pl.when(differ == 0)
-    def _():
-        packed = [in0[0, 0], in0[0, 1], in0[0, 2], in1[0, 0], in1[0, 1], in1[0, 2]]
-        for i in range(G):
-            for j in range(i, G):
-                val = packed[slot3_of(i, j)]
-                out[at(i, j)] = val
-                if i != j:
-                    out[at(j, i)] = val.T
-
-    @pl.when(differ * (1 - turned) == 1)
-    def _():
-        for i, ref in enumerate((in0, in1, in2)):
-            for j in range(G):
-                out[at(i, j)] = ref[0, j]
-
-    @pl.when(differ * turned == 1)
-    def _():
-        for i, ref in enumerate((in0, in1, in2)):
-            for j in range(G):
-                out[at(j, i)] = ref[0, j].T
+    tiles = [ref.at[0, k] for ref in (in0, in1, in2) for k in range(3 * PER)]
+
+    for sub in range(PER):
+        mat = pl.program_id(0) * PER + sub
+        turned = flip((mat // 2) % 2, x)
+
+        def at(i, j):
+            return (sub, pl.ds(i * tile, tile), pl.ds(j * tile, tile))
+
+        @pl.when(differ == 0)
+        def _():
+            for i in range(G):
+                for j in range(i, G):
+                    val = tiles[UPPER3 * sub + slot3_of(i, j)][...]
+                    out[at(i, j)] = val
+                    if i != j:
+                        out[at(j, i)] = val.T
+
+        @pl.when(differ * (1 - turned) == 1)
+        def _():
+            for i in range(G):
+                for j in range(G):
+                    out[at(i, j)] = tiles[G * G * sub + i * G + j][...]
+
+        @pl.when(differ * turned == 1)
+        def _():
+            for i in range(G):
+                for j in range(G):
+                    out[at(j, i)] = tiles[G * G * sub + i * G + j][...].T
 
 
 def solution(mesh):
@@ -386,6 +417,7 @@
                 pltpu.SemaphoreType.DMA((2,)),
                 pltpu.SemaphoreType.DMA,
                 pltpu.SemaphoreType.DMA,
+                pltpu.SemaphoreType.DMA((2, 2, G * G)),
                 pltpu.SemaphoreType.DMA,
                 pltpu.SemaphoreType.DMA,
                 pltpu.SemaphoreType.DMA,
@@ -395,10 +427,10 @@
             ),
             cost_estimate=pl.CostEstimate(flops=flops, bytes_accessed=120 * 2**20, transcendentals=0),
             name='purify',
-        )(bounds, occ, ham)
+        )(bounds.T, occ, ham)
 
         where = jnp.stack([x, x + c - 2 * x * c]).astype(jnp.int32)
-        quads = land.reshape(mats * G, G, tile, tile)
+        quads = land.reshape(mats * G // PER, G * PER, tile, tile)
 
         def part(k):
             def index(m, ref):
@@ -406,16 +438,16 @@
                 last = 0 if k == 2 else 2 * m + k
                 return off * (3 * m + k) + (1 - off) * last, 0, 0, 0
 
-            return pl.BlockSpec((1, G, tile, tile), index)
+            return pl.BlockSpec((1, G * PER, tile, tile), index)
 
         density = pl.pallas_call(
             unpack_kernel,
             out_shape=jax.ShapeDtypeStruct(ham.shape, F32),
             grid_spec=pltpu.PrefetchScalarGridSpec(
                 num_scalar_prefetch=1,
-                grid=(mats,),
+                grid=(mats // PER,),
                 in_specs=[part(0), part(1), part(2)],
-                out_specs=pl.BlockSpec((1, blk, blk), lambda m, ref: (m, 0, 0)),
+                out_specs=pl.BlockSpec((PER, blk, blk), lambda m, ref: (m, 0, 0)),
             ),
             compiler_params=pltpu.CompilerParams(vmem_limit_bytes=40 * 2**20),
             cost_estimate=pl.CostEstimate(flops=10**6, bytes_accessed=75 * 2**20, transcendentals=0),

time: 559 us -> 511 us (0.914)
  Pallas kernels: 553 us -> 507 us
    pallas_call x1, Pallas kernels: 522 us -> 478 us  [local_purify(): pl.pallas_call(main_kernel, out_shape=(jax.ShapeDtypeStruct((mats * G * G...]
where the time goes in v2:
time: 511 us
  Pallas kernels  507 us (99%)
    pallas_call x1, Pallas kernels, local_purify(): pl.pallas_call(main_kernel, out_shape=(jax.ShapeDtypeStruct((mats * G * G...  478 us
    pallas_call x1, Pallas kernels, local_purify(): pl.pallas_call(unpack_kernel, out_shape=jax.ShapeDtypeStruct(ham.shape, F...  28.8 us

profile of v2, /device:TPU:1, one launch (start us, length us, event | category | flops | bytes accessed | tf_op | source)
XLA Modules:
  0.0 510.7 jit_solution(13670671207463813457)
XLA Ops:
  0.6 0.6 pad_add_fusion.where
  1.3 478.4 %purify.1 = (f32[144,256,256]{2,1,0:T(8,128)}, f32[16,8,128]{2,1,0:T(8,128)}) custom-call(f32[2,16]{1,0:T(2,128)} %bitcast.7, s32[16]{0:T(128)} %occ.1, f32[16,768,768]{2,1,0:T(8,128)} %ham.1), custom_call_target="tpu_custom_call" | custom-call | flops 304405807104 | bytes 125829120 | tf_op jit(solution)/shard_map/purify/pallas_call | solution.py:403
  479.7 0.0 copy-start
  479.7 0.6 copy-done
  480.3 28.8 %unpack.1 = f32[16,768,768]{2,1,0:T(8,128)} custom-call(s32[2]{0:T(128)S(1)} %copy-done, f32[24,6,256,256]{3,2,1,0:T(8,128)} %bitcast.4, f32[24,6,256,256]{3,2,1,0:T(8,128)} %bitcast.5, f32[24,6,256,256]{3,2,1,0:T(8,128)} %bitcast.6), custom_call_target="tpu_custom_call" | custom-call | flops 1000000 | bytes 78643200 | tf_op jit(solution)/shard_map/unpack/pallas_call | solution.py:443
  509.1 1.6 slice_reduce_fusion
Async XLA Ops:
  479.7 0.6 copy-start

commit v3 on v2

--- a/solution.py
+++ b/solution.py
@@ -12,6 +12,7 @@
 NB = 2 * G
 UPPER = NB * (NB + 1) // 2
 UPPER3 = G * (G + 1) // 2
+OVER_X = 7
 F32 = jnp.float32
 BF16 = jnp.bfloat16
 PASSES = ((0, 2), (2, 0), (1, 1), (0, 1), (1, 0), (0, 0))
@@ -101,6 +102,12 @@
     def h_tile(mat, i, j):
         return ham.at[mat, pl.ds(i * tile, tile), pl.ds(j * tile, tile)]
 
+    def parts(diag):
+        half = tile // 2
+        if not diag:
+            return [(slice(None), slice(None))]
+        return [(pl.ds(0, half), slice(None)), (pl.ds(half, half), pl.ds(half, half))]
+
     diag_tiles = [(i, j) for i in range(G) for j in range(i, G)]
     full_tiles = [(i, j) for i in range(G) for j in range(G)]
 
@@ -112,11 +119,13 @@
             for cd in range(2):
                 for i, j in diag_tiles:
                     mat = rnd * 8 + y * 4 + (1 - x) * 2 + cd
-                    pltpu.make_async_remote_copy(
-                        h_tile(mat, i, j), stage.at[rnd, slot_of(G + i, G + j)],
-                        in_send, r_sem.at[rnd],
-                        device_id=device(y, 1 - x, cd), device_id_type=MESH,
-                    ).start()
+                    for part in parts(i == j):
+                        pltpu.make_async_remote_copy(
+                            h_tile(mat, i, j).at[part],
+                            stage.at[rnd, slot_of(G + i, G + j)].at[part],
+                            in_send, r_sem.at[rnd],
+                            device_id=device(y, 1 - x, cd), device_id_type=MESH,
+                        ).start()
             for i, j in diag_tiles:
                 pltpu.make_async_copy(
                     h_tile(rnd * 8 + own, i, j), stage.at[rnd, slot_of(i, j)], so_sem.at[rnd]
@@ -155,47 +164,78 @@
         src = stage.at[rnd, slot_of(row, col)]
         k_row, k_col = row // G, col // G
 
-        def start(dy, xd, cd, dst, sem):
-            pltpu.make_async_remote_copy(
-                src, dst, out_send, sem,
-                device_id=device(flip(y, dy), xd, cd), device_id_type=MESH,
-            ).start()
+        def start(dy, xd, cd, dst, sem, diag=False):
+            for part in parts(diag):
+                pltpu.make_async_remote_copy(
+                    src.at[part], dst.at[part], out_send, sem,
+                    device_id=device(flip(y, dy), xd, cd), device_id_type=MESH,
+                ).start()
+
+        def keep(dst, diag=False):
+            for part in parts(diag):
+                pltpu.make_async_copy(src.at[part], dst.at[part], land_sem).start()
 
         @pl.when(k_row + k_col == 1)
         def _():
             place = row * G + col - G
             dst = land.at[mat * 9 + place]
-            start(1, x, 1 - x, dst, relay_sem.at[rnd, c, place])
-            start(0, 1 - x, x, dst, land_sem)
-            pl.when(differ == 1)(lambda: pltpu.make_async_copy(src, dst, land_sem).start())
+            sem = relay_sem.at[rnd, c, place]
+
+            @pl.when(place < OVER_X)
+            def _():
+                start(1, x, 1 - x, dst, sem)
+                start(0, 1 - x, x, dst, land_sem)
+
+            @pl.when(place >= OVER_X)
+            def _():
+                start(0, 1 - x, x, dst, sem)
+                start(1, x, 1 - x, dst, land_sem)
+
+            pl.when(differ == 1)(lambda: keep(dst))
             pl.when(differ == 0)(lambda: start(0, x, 1 - x, dst, land_sem))
 
-        @pl.when(k_row == 1)
-        def _():
-            place = slot3_of(row - G, col - G)
-            start(0, 1 - x, 1 - x, land.at[mat * 6 + place], relay_sem.at[rnd, c, place])
-
-        @pl.when(k_col == 0)
-        def _():
-            dst = land.at[mat * 6 + slot3_of(row, col)]
-            start(1, x, x, dst, land_sem)
-            pl.when(differ == 0)(lambda: pltpu.make_async_copy(src, dst, land_sem).start())
-            pl.when(differ == 1)(lambda: start(0, x, x, dst, land_sem))
+        for diag in (False, True):
+            same = (row == col) if diag else (row != col)
+
+            @pl.when((k_row == 1) & same)
+            def _():
+                place = slot3_of(row - G, col - G)
+                start(0, 1 - x, 1 - x, land.at[mat * 6 + place], relay_sem.at[rnd, c, place], diag)
+
+            @pl.when((k_col == 0) & same)
+            def _():
+                dst = land.at[mat * 6 + slot3_of(row, col)]
+                start(1, x, x, dst, land_sem, diag)
+                pl.when(differ == 0)(lambda: keep(dst, diag))
+                pl.when(differ == 1)(lambda: start(0, x, x, dst, land_sem, diag))
 
     def relay(rnd, place):
-        def pass_on(first_owner, per, dev):
+        def pass_on(first_owner, per, dev, diag=False):
             for cd in range(2):
                 tile_ref = land.at[(rnd * 8 + first_owner + cd) * per + place]
-                wait_for(tile_ref, relay_sem.at[rnd, cd, place])
-                pltpu.make_async_remote_copy(
-                    tile_ref, tile_ref, out_send, land_sem, device_id=dev, device_id_type=MESH
-                ).start()
-
-        @pl.when(differ == 1)
+                whole = tile_ref.at[pl.ds(0, tile * 3 // 4)] if diag else tile_ref
+                wait_for(whole, relay_sem.at[rnd, cd, place])
+                for part in parts(diag):
+                    pltpu.make_async_remote_copy(
+                        tile_ref.at[part], tile_ref.at[part], out_send, land_sem,
+                        device_id=dev, device_id_type=MESH,
+                    ).start()
+
+        @pl.when((differ == 1) & (place < OVER_X))
         def _():
             pass_on((1 - y) * 4 + x * 2, 9, device(y, 1 - x, x))
 
-        @pl.when((differ == 0) & (place < UPPER3))
+        @pl.when((differ == 1) & (place >= OVER_X))
+        def _():
+            pass_on(y * 4 + (1 - x) * 2, 9, device(1 - y, x, c))
+
+        on_diag = (place == 0) | (place == 3) | (place == 5)
+
+        @pl.when((differ == 0) & (place < UPPER3) & on_diag)
+        def _():
+            pass_on(y * 4 + (1 - x) * 2, 6, device(1 - y, x, x), True)
+
+        @pl.when((differ == 0) & (place < UPPER3) & ~on_diag)
         def _():
             pass_on(y * 4 + (1 - x) * 2, 6, device(1 - y, x, x))
 
@@ -291,7 +331,11 @@
     def one_matrix(rnd, carry):
         mat = rnd * 8 + own
         wait_for(stage.at[rnd, pl.ds(0, 15)], so_sem.at[rnd])
-        wait_for(stage.at[rnd, pl.ds(15, 6)], r_sem.at[rnd])
+        wait_for(stage.at[rnd, pl.ds(15, 6), pl.ds(0, tile * 7 // 8)], r_sem.at[rnd])
+        half = tile // 2
+        for i in range(G, NB):
+            slot = slot_of(i, i)
+            stage[rnd, slot, half:, :half] = stage[rnd, slot, :half, half:].T
         diag_sum = fold(stage[rnd, slot_of(0, 0)] * eye)
         for i in range(1, NB):
             diag_sum += fold(stage[rnd, slot_of(i, i)] * eye)
@@ -336,66 +380,80 @@
 
     lax.fori_loop(0, 2, one_matrix, 0)
 
-    for place in range(G * G):
+    def relay_late(place, carry):
         relay(1, place)
+        return carry
+
+    lax.fori_loop(0, G * G, relay_late, 0)
     wait_for(ener.at[pl.ds(0, 14)], e_send)
     wait_for(ener, e_sem)
 
+    def wait_tiles(quarters, sem):
+        wait_for(ham.at[pl.ds(0, 16), pl.ds(0, quarters * tile // 192), :], sem)
+
     @pl.when(differ == 0)
     def _():
-        wait_for(land.at[pl.ds(0, 36)], in_send)
-        wait_for(land.at[pl.ds(0, 102)], out_send)
-        wait_for(land.at[pl.ds(0, 72)], land_sem)
+        wait_tiles(48 + 84, in_send)
+        wait_tiles(4 * 96, out_send)
+        wait_tiles(4 * 63, land_sem)
 
     @pl.when(differ == 1)
     def _():
-        wait_for(land.at[pl.ds(0, 18)], in_send)
-        wait_for(land.at[pl.ds(0, 108)], out_send)
-        wait_for(land.at[pl.ds(0, 108)], land_sem)
+        wait_tiles(4 * 18, in_send)
+        wait_tiles(414, out_send)
+        wait_tiles(4 * 108, land_sem)
 
 
 PER = 2
 
 
-def unpack_kernel(where, in0, in1, in2, out):
+def unpack_kernel(in0, in1, in2, out):
     tile = in0.shape[2]
-    x, differ = where[0], where[1]
+    half = tile // 2
+    x, c = lax.axis_index('row'), lax.axis_index('col')
+    differ = flip(x, c)
     tiles = [ref.at[0, k] for ref in (in0, in1, in2) for k in range(3 * PER)]
 
     for sub in range(PER):
         mat = pl.program_id(0) * PER + sub
         turned = flip((mat // 2) % 2, x)
 
-        def at(i, j):
-            return (sub, pl.ds(i * tile, tile), pl.ds(j * tile, tile))
+        def write(i, j, val):
+            rows, cols = val.shape
+            out[sub, pl.ds(i * half, rows), pl.ds(j * half, cols)] = val
 
         @pl.when(differ == 0)
         def _():
             for i in range(G):
                 for j in range(i, G):
-                    val = tiles[UPPER3 * sub + slot3_of(i, j)][...]
-                    out[at(i, j)] = val
-                    if i != j:
-                        out[at(j, i)] = val.T
+                    ref = tiles[UPPER3 * sub + slot3_of(i, j)]
+                    if i == j:
+                        top = ref[:half, :]
+                        write(2 * i, 2 * i, top)
+                        write(2 * i + 1, 2 * i, top[:, half:].T)
+                        write(2 * i + 1, 2 * i + 1, ref[half:, half:])
+                    else:
+                        val = ref[...]
+                        write(2 * i, 2 * j, val)
+                        write(2 * j, 2 * i, val.T)
 
         @pl.when(differ * (1 - turned) == 1)
         def _():
             for i in range(G):
                 for j in range(G):
-                    out[at(i, j)] = tiles[G * G * sub + i * G + j][...]
+                    write(2 * i, 2 * j, tiles[G * G * sub + i * G + j][...])
 
         @pl.when(differ * turned == 1)
         def _():
             for i in range(G):
                 for j in range(G):
-                    out[at(j, i)] = tiles[G * G * sub + i * G + j][...].T
+                    write(2 * j, 2 * i, tiles[G * G * sub + i * G + j][...].T)
 
 
 def solution(mesh):
     def local_purify(ham, bounds, occ):
         mats, blk, _ = ham.shape
         tile = blk // G
-        x, c = lax.axis_index('row'), lax.axis_index('col')
         any_spec = pl.BlockSpec(memory_space=pltpu.HBM)
         smem = pl.BlockSpec(memory_space=pltpu.SMEM)
         limb = pltpu.VMEM((3, NB, NB, tile, tile), BF16)
@@ -429,12 +487,11 @@
             name='purify',
         )(bounds.T, occ, ham)
 
-        where = jnp.stack([x, x + c - 2 * x * c]).astype(jnp.int32)
         quads = land.reshape(mats * G // PER, G * PER, tile, tile)
 
         def part(k):
-            def index(m, ref):
-                off = ref[1]
+            def index(m):
+                off = flip(lax.axis_index('row'), lax.axis_index('col'))
                 last = 0 if k == 2 else 2 * m + k
                 return off * (3 * m + k) + (1 - off) * last, 0, 0, 0
 
@@ -443,16 +500,13 @@
         density = pl.pallas_call(
             unpack_kernel,
             out_shape=jax.ShapeDtypeStruct(ham.shape, F32),
-            grid_spec=pltpu.PrefetchScalarGridSpec(
-                num_scalar_prefetch=1,
-                grid=(mats // PER,),
-                in_specs=[part(0), part(1), part(2)],
-                out_specs=pl.BlockSpec((PER, blk, blk), lambda m, ref: (m, 0, 0)),
-            ),
+            grid=(mats // PER,),
+            in_specs=[part(0), part(1), part(2)],
+            out_specs=pl.BlockSpec((PER, blk, blk), lambda m: (m, 0, 0)),
             compiler_params=pltpu.CompilerParams(vmem_limit_bytes=40 * 2**20),
             cost_estimate=pl.CostEstimate(flops=10**6, bytes_accessed=75 * 2**20, transcendentals=0),
             name='unpack',
-        )(where, quads, quads, quads)
+        )(quads, quads, quads)
         return density, ener[:, 0, 0]
 
     mat_spec = P('spin', 'row', 'col')

time: 511 us -> 490 us (0.959)
  Pallas kernels: 507 us -> 487 us
    pallas_call x1, Pallas kernels: 478 us -> 459 us  [local_purify(): pl.pallas_call(main_kernel, out_shape=(jax.ShapeDtypeStruct((mats * G * G...]
where the time goes in v3:
time: 490 us
  Pallas kernels  487 us (99%)
    pallas_call x1, Pallas kernels, local_purify(): pl.pallas_call(main_kernel, out_shape=(jax.ShapeDtypeStruct((mats * G * G...  459 us
    pallas_call x1, Pallas kernels, local_purify(): pl.pallas_call(unpack_kernel, out_shape=jax.ShapeDtypeStruct(ham.shape, F...  28.3 us

profile of v3, /device:TPU:1, one launch (start us, length us, event | category | flops | bytes accessed | tf_op | source)
XLA Modules:
  0.0 489.5 jit_solution(13613294631624566135)
XLA Ops:
  0.6 459.1 %purify.1 = (f32[144,256,256]{2,1,0:T(8,128)}, f32[16,8,128]{2,1,0:T(8,128)}) custom-call(f32[2,16]{1,0:T(2,128)} %bitcast.5, s32[16]{0:T(128)} %occ.1, f32[16,768,768]{2,1,0:T(8,128)} %ham.1), custom_call_target="tpu_custom_call" | custom-call | flops 304405807104 | bytes 125829120 | tf_op jit(solution)/shard_map/purify/pallas_call | solution.py:461
  459.7 28.3 %unpack.1 = f32[16,768,768]{2,1,0:T(8,128)} custom-call(f32[24,6,256,256]{3,2,1,0:T(8,128)} %bitcast.2, f32[24,6,256,256]{3,2,1,0:T(8,128)} %bitcast.3, f32[24,6,256,256]{3,2,1,0:T(8,128)} %bitcast.4), custom_call_target="tpu_custom_call" | custom-call | flops 1000000 | bytes 78643200 | tf_op jit(solution)/shard_map/unpack/pallas_call | solution.py:500
  488.0 1.6 slice_reduce_fusion

commit v4 on v3

--- a/solution.py
+++ b/solution.py
@@ -79,7 +79,7 @@
 def main_kernel(
     bounds, occ, ham, land, ener,
     buf_a, buf_b, buf_c, stage, sums, e_vec,
-    so_sem, r_sem, in_send, land_sem, relay_sem, out_send, e_sem, e_send,
+    so_sem, r_sem, in_send, aid_sem, aid_send, land_sem, relay_sem, out_send, e_sem, e_send,
 ):
     tile = stage.shape[2]
     order = NB * tile
@@ -109,48 +109,58 @@
         return [(pl.ds(0, half), slice(None)), (pl.ds(half, half), pl.ds(half, half))]
 
     diag_tiles = [(i, j) for i in range(G) for j in range(i, G)]
-    full_tiles = [(i, j) for i in range(G) for j in range(G)]
-
-    def send_in(rnd, carry):
-        other = own + 1 - 2 * c
+
+    def send_in(e, carry):
+        late = e // 3
+        aid = (e % 3) % 2 * (1 - late)
+        cd = (1 - late) * ((e + 1) // 2) + late * (e - 3)
+        mat = 8 * (aid + late) + cd * (1 - aid) + y * 4
+        put_in = 2 * aid + late
 
         @pl.when(differ == 0)
         def _():
-            for cd in range(2):
-                for i, j in diag_tiles:
-                    mat = rnd * 8 + y * 4 + (1 - x) * 2 + cd
-                    for part in parts(i == j):
-                        pltpu.make_async_remote_copy(
-                            h_tile(mat, i, j).at[part],
-                            stage.at[rnd, slot_of(G + i, G + j)].at[part],
-                            in_send, r_sem.at[rnd],
-                            device_id=device(y, 1 - x, cd), device_id_type=MESH,
-                        ).start()
             for i, j in diag_tiles:
-                pltpu.make_async_copy(
-                    h_tile(rnd * 8 + own, i, j), stage.at[rnd, slot_of(i, j)], so_sem.at[rnd]
+                for part in parts(i == j):
+                    pltpu.make_async_remote_copy(
+                        h_tile(mat + (1 - x) * 2, i, j).at[part],
+                        stage.at[put_in, slot_of(G + i, G + j)].at[part],
+                        in_send, r_sem.at[put_in],
+                        device_id=device(y, 1 - x, cd), device_id_type=MESH,
+                    ).start()
+
+        def near(tiles, shift):
+            for i, j in tiles:
+                near_tile(i, j, shift)
+
+        def near_row(i, carry_):
+            for j in range(G):
+                near_tile(i, j, G)
+            return carry_
+
+        def near_tile(i, j, shift):
+            src = h_tile(mat + x * 2, i, j)
+            dst = stage.at[put_in, slot_of(i, shift + j)]
+
+            @pl.when(cd == c)
+            def _():
+                pltpu.make_async_copy(src, dst, so_sem.at[put_in]).start()
+
+            @pl.when(cd != c)
+            def _():
+                pltpu.make_async_remote_copy(
+                    src, dst, in_send, so_sem.at[put_in],
+                    device_id=device(y, x, cd), device_id_type=MESH,
                 ).start()
-                pltpu.make_async_remote_copy(
-                    h_tile(rnd * 8 + other, i, j), stage.at[rnd, slot_of(i, j)],
-                    in_send, so_sem.at[rnd],
-                    device_id=device(y, x, 1 - c), device_id_type=MESH,
-                ).start()
+
+        pl.when(differ == 0)(lambda: near(diag_tiles, 0))
 
         @pl.when(differ == 1)
         def _():
-            for i, j in full_tiles:
-                pltpu.make_async_copy(
-                    h_tile(rnd * 8 + own, i, j), stage.at[rnd, slot_of(i, G + j)], so_sem.at[rnd]
-                ).start()
-                pltpu.make_async_remote_copy(
-                    h_tile(rnd * 8 + other, i, j), stage.at[rnd, slot_of(i, G + j)],
-                    in_send, so_sem.at[rnd],
-                    device_id=device(y, x, 1 - c), device_id_type=MESH,
-                ).start()
+            lax.fori_loop(0, G, near_row, 0)
 
         return carry
 
-    lax.fori_loop(0, 2, send_in, 0)
+    lax.fori_loop(0, 5, send_in, 0)
 
     def wait_for(ref, sem):
         pltpu.make_async_copy(ref, ref, sem).wait()
@@ -239,8 +249,20 @@
         def _():
             pass_on(y * 4 + (1 - x) * 2, 6, device(1 - y, x, x))
 
-    def relay_early(rnd, turn):
-        pl.when((rnd == 1) & (turn >= 3) & (turn < 3 + G * G))(lambda: relay(0, turn - 3))
+    def relay_early(job, turn):
+        one = (c == 1) & (turn >= 1) & (turn < 1 + G * G)
+        two = (c == 0) & (turn >= 9) & (turn < 14)
+
+        @pl.when((job == 2) & (one | two))
+        def _():
+            low = c * (turn - 1) + (1 - c) * 2 * (turn - 9)
+            high = low + 1 + (1 - c) * (1 - turn // 13)
+
+            def body(place, carry):
+                relay(0, place)
+                return carry
+
+            lax.fori_loop(low, high, body, 0)
 
     def tiles_of(turn):
         out = []
@@ -251,9 +273,28 @@
         out.append((turn, turn + 3, False))
         return out
 
-    def square(src, rnd, before):
+    def unit(v, step):
+        late = (v + 3) // 6
+        half = (v - 3) % 2
+        base = G * (1 - (v - 3) // 2)
+        row = base + half * (1 + step // 2)
+        col = base + (1 - half) * step + half * (1 + (step + 1) // 2)
+        return row * late + v * (1 - late), col * late + (G + step) * (1 - late)
+
+    def send_aid(v):
+        for row, col, _ in tiles_of(v):
+            ref = stage.at[2, slot_of(row, col)]
+            pltpu.make_async_remote_copy(
+                ref, ref, aid_send, aid_sem, device_id=device(y, x, 0), device_id_type=MESH
+            ).start()
+
+    def square(src, job, before, may_aid):
+        own_job = (job + 1) // 2
+
         def turn(v, carry):
-            relay_early(rnd, before + v)
+            relay_early(job, before + v)
+            if may_aid:
+                pl.when((job == 0) & (v > 0))(lambda: send_aid(v - 1))
             for row, col, diag in tiles_of(v):
                 if diag:
                     cross = chain(src, src, row, col, ((0, 2), (0, 1)))
@@ -262,11 +303,29 @@
                 else:
                     val = chain(src, src, row, col, PASSES)
                 put(buf_b, row, col, val, diag)
+                if may_aid:
+                    stage[2, slot_of(row, col) * (1 - own_job) + UPPER * own_job] = val
                 sums[2] += fold(val * get(src, row, col)) * (1.0 if diag else 2.0)
             return carry
 
         sums[2] = jnp.zeros_like(sums[2])
         lax.fori_loop(0, 3, turn, 0)
+        if may_aid:
+            pl.when(job == 0)(lambda: send_aid(2))
+
+    def absorb():
+        wait_for(stage.at[2, pl.ds(0, UPPER)], aid_sem)
+        sums[2] = jnp.zeros_like(sums[2])
+
+        def turn(v, carry):
+            for step in range(3):
+                row, col = unit(v, step)
+                val = stage[2, slot_of(row, col)]
+                put(buf_b, row, col, val, False)
+                sums[2] += fold(val * get(buf_a, row, col)) * jnp.where(row == col, 1.0, 2.0)
+            return carry
+
+        lax.fori_loop(0, 7, turn, 0)
 
     def coefs():
         t1, t2, t3 = total(sums[0]), total(sums[1]), total(sums[2])
@@ -283,12 +342,12 @@
         acc = chain(buf_b, src, row, col, PASSES)
         return co[0] * get(src, row, col) + co[1] * get(buf_b, row, col) - co[2] * acc
 
-    def cube(src, dst, rnd, before):
+    def cube(src, dst, job, before):
         co = coefs()
         sums[0:2] = jnp.zeros_like(sums[0:2])
 
         def turn(v, carry):
-            relay_early(rnd, before + v)
+            relay_early(job, before + v)
             for row, col, diag in tiles_of(v):
                 val = combine(src, row, col, co)
                 put(dst, row, col, val, diag)
@@ -300,14 +359,6 @@
     def cube_last(src, rnd):
         co = coefs()
         sums[0] = jnp.zeros_like(sums[0])
-
-        def unit(v, step):
-            late = (v + 3) // 6
-            half = (v - 3) % 2
-            base = G * (1 - (v - 3) // 2)
-            row = base + half * (1 + step // 2)
-            col = base + (1 - half) * step + half * (1 + (step + 1) // 2)
-            return row * late + v * (1 - late), col * late + (G + step) * (1 - late)
 
         def turn(v, carry):
             @pl.when(v > 0)
@@ -328,17 +379,24 @@
         for step in range(3):
             send_out(rnd, *unit(6, step))
 
-    def one_matrix(rnd, carry):
-        mat = rnd * 8 + own
-        wait_for(stage.at[rnd, pl.ds(0, 15)], so_sem.at[rnd])
-        wait_for(stage.at[rnd, pl.ds(15, 6), pl.ds(0, tile * 7 // 8)], r_sem.at[rnd])
+    def one_job(job, carry):
+        pl.when((job > 0) | (c == 1))(lambda: run_job(job))
+        return carry
+
+    def run_job(job):
+        own_job = (job + 1) // 2
+        rnd = job - 1
+        put_in = (job + 2) % 3
+        mat = own_job * (rnd * 8 + own) + (1 - own_job) * (8 + own - 1)
+        wait_for(stage.at[put_in, pl.ds(0, 15)], so_sem.at[put_in])
+        wait_for(stage.at[put_in, pl.ds(15, 6), pl.ds(0, tile * 7 // 8)], r_sem.at[put_in])
         half = tile // 2
         for i in range(G, NB):
             slot = slot_of(i, i)
-            stage[rnd, slot, half:, :half] = stage[rnd, slot, :half, half:].T
-        diag_sum = fold(stage[rnd, slot_of(0, 0)] * eye)
+            stage[put_in, slot, half:, :half] = stage[put_in, slot, :half, half:].T
+        diag_sum = fold(stage[put_in, slot_of(0, 0)] * eye)
         for i in range(1, NB):
-            diag_sum += fold(stage[rnd, slot_of(i, i)] * eye)
+            diag_sum += fold(stage[put_in, slot_of(i, i)] * eye)
         mean = total(diag_sum) / order
         filled = occ[mat].astype(F32)
         scale = jnp.minimum(
@@ -349,25 +407,35 @@
         sums[0:2] = jnp.zeros_like(sums[0:2])
 
         def first(v, c_):
-            for row, col, diag in tiles_of(v):
-                val = stage[rnd, slot_of(row, col)] * -slope
-                if diag:
-                    val = val + on_diag * eye
-                put(buf_a, row, col, val, diag)
-                count(val, diag)
+            for step in range(3):
+                row, col = unit(v, step)
+                one = jnp.where(row == col, 1.0, 0.0)
+                val = stage[put_in, slot_of(row, col)] * -slope + (on_diag * one) * eye
+                put(buf_a, row, col, val, False)
+                sums[0] += fold(val * eye) * one
+                sums[1] += fold(val * val) * (2.0 - one)
             return c_
 
-        lax.fori_loop(0, 3, first, 0)
+        lax.fori_loop(0, 7, first, 0)
+        given = (job == 2) & (c == 0)
+        mine = job > 0
 
         def step(s, c_):
-            pl.when(s != 1)(lambda: square(buf_a, rnd, 6 * s))
-            pl.when(s == 1)(lambda: square(buf_c, rnd, 6))
-            pl.when(s == 0)(lambda: cube(buf_a, buf_c, rnd, 3))
-            pl.when(s == 1)(lambda: cube(buf_c, buf_a, rnd, 9))
-            pl.when(s == 2)(lambda: cube_last(buf_a, rnd))
+            @pl.when(((s == 0) & ~given) | ((s == 2) & mine))
+            def _():
+                square(buf_a, job, 6 * s, True)
+
+            pl.when((s == 0) & given)(absorb)
+            pl.when((s == 1) & mine)(lambda: square(buf_c, job, 6, False))
+            pl.when((s == 0) & mine)(lambda: cube(buf_a, buf_c, job, 3))
+            pl.when((s == 1) & mine)(lambda: cube(buf_c, buf_a, job, 9))
+            pl.when((s == 2) & mine)(lambda: finish(rnd, mat))
             return c_
 
         lax.fori_loop(0, STEPS, step, 0)
+
+    def finish(rnd, mat):
+        cube_last(buf_a, rnd)
         e_vec[rnd] = jnp.broadcast_to(2.0 * total(sums[0]), e_vec.shape[1:])
         for k in range(1, 8):
             pltpu.make_async_remote_copy(
@@ -376,9 +444,8 @@
                 device_id_type=MESH,
             ).start()
         pltpu.make_async_copy(e_vec.at[rnd], ener.at[mat], e_sem).start()
-        return carry
-
-    lax.fori_loop(0, 2, one_matrix, 0)
+
+    lax.fori_loop(0, 3, one_job, 0)
 
     def relay_late(place, carry):
         relay(1, place)
@@ -389,17 +456,24 @@
     wait_for(ener, e_sem)
 
     def wait_tiles(quarters, sem):
-        wait_for(ham.at[pl.ds(0, 16), pl.ds(0, quarters * tile // 192), :], sem)
+        lead = 8 if quarters <= 288 else 16
+        wait_for(ham.at[pl.ds(0, lead), pl.ds(0, quarters * tile // (12 * lead)), :], sem)
+
+    @pl.when(c == 1)
+    def _():
+        wait_for(stage.at[2, pl.ds(0, UPPER)], aid_send)
 
     @pl.when(differ == 0)
     def _():
-        wait_tiles(48 + 84, in_send)
+        pl.when(c == 0)(lambda: wait_tiles(105 + 72, in_send))
+        pl.when(c == 1)(lambda: wait_tiles(105 + 48, in_send))
         wait_tiles(4 * 96, out_send)
         wait_tiles(4 * 63, land_sem)
 
     @pl.when(differ == 1)
     def _():
-        wait_tiles(4 * 18, in_send)
+        pl.when(c == 0)(lambda: wait_tiles(108, in_send))
+        pl.when(c == 1)(lambda: wait_tiles(72, in_send))
         wait_tiles(414, out_send)
         wait_tiles(4 * 108, land_sem)
 
@@ -468,11 +542,13 @@
             out_specs=(any_spec, any_spec),
             scratch_shapes=[
                 limb, limb, limb,
-                pltpu.VMEM((2, UPPER, tile, tile), F32),
+                pltpu.VMEM((3, UPPER + 1, tile, tile), F32),
                 pltpu.VMEM((3, 8, tile), F32),
                 pltpu.VMEM((2, 8, 128), F32),
-                pltpu.SemaphoreType.DMA((2,)),
-                pltpu.SemaphoreType.DMA((2,)),
+                pltpu.SemaphoreType.DMA((3,)),
+                pltpu.SemaphoreType.DMA((3,)),
+                pltpu.SemaphoreType.DMA,
+                pltpu.SemaphoreType.DMA,
                 pltpu.SemaphoreType.DMA,
                 pltpu.SemaphoreType.DMA,
                 pltpu.SemaphoreType.DMA((2, 2, G * G)),

time: 490 us -> 483 us (0.986)
  Pallas kernels: 487 us -> 480 us
    pallas_call x1, Pallas kernels: 459 us -> 452 us  [local_purify(): pl.pallas_call(main_kernel, out_shape=(jax.ShapeDtypeStruct((mats * G * G...]
where the time goes in v4:
time: 483 us; the launch traced here: 482 us
  Pallas kernels  480 us (99%)
    pallas_call x1, Pallas kernels, local_purify(): pl.pallas_call(main_kernel, out_shape=(jax.ShapeDtypeStruct((mats * G * G...  452 us
    pallas_call x1, Pallas kernels, local_purify(): pl.pallas_call(unpack_kernel, out_shape=jax.ShapeDtypeStruct(ham.shape, F...  28.3 us

profile of v4, /device:TPU:1, one launch (start us, length us, event | category | flops | bytes accessed | tf_op | source)
XLA Modules:
  0.0 482.4 jit_solution(3868886593102979592)
XLA Ops:
  0.6 451.9 %purify.1 = (f32[144,256,256]{2,1,0:T(8,128)}, f32[16,8,128]{2,1,0:T(8,128)}) custom-call(f32[2,16]{1,0:T(2,128)} %bitcast.5, s32[16]{0:T(128)} %occ.1, f32[16,768,768]{2,1,0:T(8,128)} %ham.1), custom_call_target="tpu_custom_call" | custom-call | flops 304405807104 | bytes 125829120 | tf_op jit(solution)/shard_map/purify/pallas_call | solution.py:535
  452.6 28.3 %unpack.1 = f32[16,768,768]{2,1,0:T(8,128)} custom-call(f32[24,6,256,256]{3,2,1,0:T(8,128)} %bitcast.2, f32[24,6,256,256]{3,2,1,0:T(8,128)} %bitcast.3, f32[24,6,256,256]{3,2,1,0:T(8,128)} %bitcast.4), custom_call_target="tpu_custom_call" | custom-call | flops 1000000 | bytes 78643200 | tf_op jit(solution)/shard_map/unpack/pallas_call | solution.py:576
  480.9 1.6 slice_reduce_fusion

commit v5 on v4

--- a/solution.py
+++ b/solution.py
@@ -219,35 +219,30 @@
                 pl.when(differ == 0)(lambda: keep(dst, diag))
                 pl.when(differ == 1)(lambda: start(0, x, x, dst, land_sem, diag))
 
-    def relay(rnd, place):
-        def pass_on(first_owner, per, dev, diag=False):
-            for cd in range(2):
-                tile_ref = land.at[(rnd * 8 + first_owner + cd) * per + place]
-                whole = tile_ref.at[pl.ds(0, tile * 3 // 4)] if diag else tile_ref
-                wait_for(whole, relay_sem.at[rnd, cd, place])
-                for part in parts(diag):
-                    pltpu.make_async_remote_copy(
-                        tile_ref.at[part], tile_ref.at[part], out_send, land_sem,
-                        device_id=dev, device_id_type=MESH,
-                    ).start()
-
-        @pl.when((differ == 1) & (place < OVER_X))
-        def _():
-            pass_on((1 - y) * 4 + x * 2, 9, device(y, 1 - x, x))
-
-        @pl.when((differ == 1) & (place >= OVER_X))
-        def _():
-            pass_on(y * 4 + (1 - x) * 2, 9, device(1 - y, x, c))
-
-        on_diag = (place == 0) | (place == 3) | (place == 5)
-
-        @pl.when((differ == 0) & (place < UPPER3) & on_diag)
-        def _():
-            pass_on(y * 4 + (1 - x) * 2, 6, device(1 - y, x, x), True)
-
-        @pl.when((differ == 0) & (place < UPPER3) & ~on_diag)
-        def _():
-            pass_on(y * 4 + (1 - x) * 2, 6, device(1 - y, x, x))
+    def relay(rnd, cd, place):
+        over_x = differ * (1 - place // OVER_X)
+        owner = over_x * ((1 - y) * 4 + x * 2) + (1 - over_x) * (y * 4 + (1 - x) * 2) + cd
+        dev = device(flip(y, 1 - over_x), flip(x, over_x), over_x * x + (1 - over_x) * c)
+        tile_ref = land.at[(rnd * 8 + owner) * (UPPER3 + 3 * differ) + place]
+
+        def pass_on(whole, diag):
+            wait_for(whole, relay_sem.at[rnd, cd, place])
+            for part in parts(diag):
+                pltpu.make_async_remote_copy(
+                    tile_ref.at[part], tile_ref.at[part], out_send, land_sem,
+                    device_id=dev, device_id_type=MESH,
+                ).start()
+
+        on_diag = (differ == 0) & ((place == 0) | (place == 3) | (place == 5))
+        pl.when(on_diag)(lambda: pass_on(tile_ref.at[pl.ds(0, tile * 3 // 4)], True))
+        pl.when(~on_diag & (place < UPPER3 + 3 * differ))(lambda: pass_on(tile_ref, False))
+
+    def relays(rnd, cd, low, count):
+        def body(k, carry):
+            relay(rnd, cd, low + k)
+            return carry
+
+        lax.fori_loop(0, count, body, 0)
 
     def relay_early(job, turn):
         one = (c == 1) & (turn >= 1) & (turn < 1 + G * G)
@@ -256,13 +251,24 @@
         @pl.when((job == 2) & (one | two))
         def _():
             low = c * (turn - 1) + (1 - c) * 2 * (turn - 9)
-            high = low + 1 + (1 - c) * (1 - turn // 13)
-
-            def body(place, carry):
-                relay(0, place)
+            count = 1 + (1 - c) * (1 - turn // 13)
+
+            def body(k, carry):
+                relay(0, k % 2, low + k // 2)
                 return carry
 
-            lax.fori_loop(low, high, body, 0)
+            lax.fori_loop(0, 2 * count, body, 0)
+
+        @pl.when((job == 2) & (c == 1) & (turn >= 12))
+        def _():
+            later = (turn - 11) // 2
+            low = differ * later * (2 * turn - 23)
+            relays(1, 0, low, differ * (3 - later) + (1 - differ) * (turn // 14))
+
+    def relay_last(rnd, v):
+        @pl.when((rnd == 1) & (c == 1) & (v >= 1) & (v < UPPER3 - 3 * differ))
+        def _():
+            relays(1, 0, v + 6 * differ, 1)
 
     def tiles_of(turn):
         out = []
@@ -365,6 +371,8 @@
             def _():
                 for step in range(3):
                     send_out(rnd, *unit(v - 1, step))
+
+            relay_last(rnd, v)
 
             for step in range(3):
                 row, col = unit(v, step)
@@ -436,7 +444,8 @@
 
     def finish(rnd, mat):
         cube_last(buf_a, rnd)
-        e_vec[rnd] = jnp.broadcast_to(2.0 * total(sums[0]), e_vec.shape[1:])
+        lane = lax.broadcasted_iota(jnp.int32, e_vec.shape[1:], 1)
+        e_vec[rnd] = jnp.where(lane == mat, 2.0 * total(sums[0]), 0.0)
         for k in range(1, 8):
             pltpu.make_async_remote_copy(
                 e_vec.at[rnd], ener.at[mat], e_send, e_sem,
@@ -447,11 +456,8 @@
 
     lax.fori_loop(0, 3, one_job, 0)
 
-    def relay_late(place, carry):
-        relay(1, place)
-        return carry
-
-    lax.fori_loop(0, G * G, relay_late, 0)
+    pl.when(c == 0)(lambda: relays(1, 0, 0, G * G))
+    relays(1, 1, 0, G * G)
     wait_for(ener.at[pl.ds(0, 14)], e_send)
     wait_for(ener, e_sem)
 
@@ -478,36 +484,62 @@
         wait_tiles(4 * 108, land_sem)
 
 
-PER = 2
-
-
-def unpack_kernel(in0, in1, in2, out):
-    tile = in0.shape[2]
+RING = 4
+
+
+def unpack_kernel(land, ener, out, energy, held, block, in_sem, out_sem):
+    mats, tile = out.shape[0], land.shape[1]
     half = tile // 2
     x, c = lax.axis_index('row'), lax.axis_index('col')
     differ = flip(x, c)
-    tiles = [ref.at[0, k] for ref in (in0, in1, in2) for k in range(3 * PER)]
-
-    for sub in range(PER):
-        mat = pl.program_id(0) * PER + sub
+
+    def load(mat, act):
+        slot = mat % RING
+        for kind, count in ((0, UPPER3), (1, G * G)):
+
+            @pl.when(differ == kind)
+            def _():
+                act(
+                    pltpu.make_async_copy(
+                        land.at[pl.ds(mat * count, count)],
+                        held.at[slot, pl.ds(0, count)],
+                        in_sem.at[slot],
+                    )
+                )
+
+    def store(mat):
+        slot = mat % RING
+        return pltpu.make_async_copy(block.at[slot], out.at[mat], out_sem.at[slot])
+
+    def prime(mat, carry):
+        load(mat, lambda copy: copy.start())
+        return carry
+
+    lax.fori_loop(0, RING, prime, 0)
+    energy[...] = jnp.sum(ener[...], axis=0)[0, : energy.shape[0]]
+
+    def turn(mat, carry):
+        slot = mat % RING
         turned = flip((mat // 2) % 2, x)
+        load(mat, lambda copy: copy.wait())
+        pl.when(mat >= RING)(lambda: store(mat - RING).wait())
 
         def write(i, j, val):
             rows, cols = val.shape
-            out[sub, pl.ds(i * half, rows), pl.ds(j * half, cols)] = val
+            block[slot, pl.ds(i * half, rows), pl.ds(j * half, cols)] = val
 
         @pl.when(differ == 0)
         def _():
             for i in range(G):
                 for j in range(i, G):
-                    ref = tiles[UPPER3 * sub + slot3_of(i, j)]
+                    place = slot3_of(i, j)
                     if i == j:
-                        top = ref[:half, :]
+                        top = held[slot, place, :half, :]
                         write(2 * i, 2 * i, top)
                         write(2 * i + 1, 2 * i, top[:, half:].T)
-                        write(2 * i + 1, 2 * i + 1, ref[half:, half:])
+                        write(2 * i + 1, 2 * i + 1, held[slot, place, half:, half:])
                     else:
-                        val = ref[...]
+                        val = held[slot, place]
                         write(2 * i, 2 * j, val)
                         write(2 * j, 2 * i, val.T)
 
@@ -515,13 +547,21 @@
         def _():
             for i in range(G):
                 for j in range(G):
-                    write(2 * i, 2 * j, tiles[G * G * sub + i * G + j][...])
+                    write(2 * i, 2 * j, held[slot, i * G + j])
 
         @pl.when(differ * turned == 1)
         def _():
             for i in range(G):
                 for j in range(G):
-                    write(2 * j, 2 * i, tiles[G * G * sub + i * G + j][...].T)
+                    write(2 * j, 2 * i, held[slot, i * G + j].T)
+
+        store(mat).start()
+        pl.when(mat + RING < mats)(lambda: load(mat + RING, lambda copy: copy.start()))
+        return carry
+
+    lax.fori_loop(0, mats, turn, 0)
+    for mat in range(mats - RING, mats):
+        store(mat).wait()
 
 
 def solution(mesh):
@@ -563,27 +603,24 @@
             name='purify',
         )(bounds.T, occ, ham)
 
-        quads = land.reshape(mats * G // PER, G * PER, tile, tile)
-
-        def part(k):
-            def index(m):
-                off = flip(lax.axis_index('row'), lax.axis_index('col'))
-                last = 0 if k == 2 else 2 * m + k
-                return off * (3 * m + k) + (1 - off) * last, 0, 0, 0
-
-            return pl.BlockSpec((1, G * PER, tile, tile), index)
-
-        density = pl.pallas_call(
+        return pl.pallas_call(
             unpack_kernel,
-            out_shape=jax.ShapeDtypeStruct(ham.shape, F32),
-            grid=(mats // PER,),
-            in_specs=[part(0), part(1), part(2)],
-            out_specs=pl.BlockSpec((PER, blk, blk), lambda m: (m, 0, 0)),
+            out_shape=(
+                jax.ShapeDtypeStruct(ham.shape, F32),
+                jax.ShapeDtypeStruct((mats,), F32),
+            ),
+            in_specs=[any_spec, pl.BlockSpec(memory_space=pltpu.VMEM)],
+            out_specs=(any_spec, pl.BlockSpec(memory_space=pltpu.VMEM)),
+            scratch_shapes=[
+                pltpu.VMEM((RING, G * G, tile, tile), F32),
+                pltpu.VMEM((RING, blk, blk), F32),
+                pltpu.SemaphoreType.DMA((RING,)),
+                pltpu.SemaphoreType.DMA((RING,)),
+            ],
             compiler_params=pltpu.CompilerParams(vmem_limit_bytes=40 * 2**20),
             cost_estimate=pl.CostEstimate(flops=10**6, bytes_accessed=75 * 2**20, transcendentals=0),
             name='unpack',
-        )(quads, quads, quads)
-        return density, ener[:, 0, 0]
+        )(land, ener)
 
     mat_spec = P('spin', 'row', 'col')
     return jax.shard_map(

time: 483 us -> 471 us (0.975); the launches traced: 482 us -> 464 us
  Pallas kernels: 480 us -> 462 us
    pallas_call x1, Pallas kernels: 452 us -> 436 us  [local_purify(): pl.pallas_call(main_kernel, out_shape=(jax.ShapeDtypeStruct((mats * G * G...]
where the time goes in v5:
time: 471 us; the launch traced here: 464 us
  Pallas kernels  462 us (98%)
    pallas_call x1, Pallas kernels, local_purify(): pl.pallas_call(main_kernel, out_shape=(jax.ShapeDtypeStruct((mats * G * G...  436 us
    pallas_call x1, Pallas kernels, local_purify(): pl.pallas_call(unpack_kernel, out_shape=(jax.ShapeDtypeStruct(ham.shape,...  26.2 us

profile of v5, /device:TPU:1, one launch (start us, length us, event | category | flops | bytes accessed | tf_op | source)
XLA Modules:
  0.0 463.5 jit_solution(16906222650410020231)
XLA Ops:
  0.6 435.8 %purify.1 = (f32[144,256,256]{2,1,0:T(8,128)}, f32[16,8,128]{2,1,0:T(8,128)}) custom-call(f32[2,16]{1,0:T(2,128)} %bitcast.1, s32[16]{0:T(128)} %occ.1, f32[16,768,768]{2,1,0:T(8,128)} %ham.1), custom_call_target="tpu_custom_call" | custom-call | flops 304405807104 | bytes 125829120 | tf_op jit(solution)/shard_map/purify/pallas_call | solution.py:575
  436.4 0.0 copy-start
  436.4 0.8 copy-done
  437.3 26.2 %unpack.1 = (f32[16,768,768]{2,1,0:T(8,128)}, f32[16]{0:T(128)}) custom-call(f32[144,256,256]{2,1,0:T(8,128)} %get-tuple-element.4.land, f32[16,8,128]{2,1,0:T(8,128)S(1)} %copy-done), custom_call_target="tpu_custom_call" | custom-call | flops 1000000 | bytes 78643200 | tf_op jit(solution)/shard_map/unpack/pallas_call | solution.py:606
Async XLA Ops:
  436.4 0.8 copy-start

commit v6 on v5

--- a/solution.py
+++ b/solution.py
@@ -12,7 +12,7 @@
 NB = 2 * G
 UPPER = NB * (NB + 1) // 2
 UPPER3 = G * (G + 1) // 2
-OVER_X = 7
+OVER_X = 8
 F32 = jnp.float32
 BF16 = jnp.bfloat16
 PASSES = ((0, 2), (2, 0), (1, 1), (0, 1), (1, 0), (0, 0))
@@ -277,7 +277,7 @@
             for step in range(3):
                 out.append((*upper_tile(row, step), step == 0))
         out.append((turn, turn + 3, False))
-        return out
+        return sorted(out, key=lambda item: item[2])
 
     def unit(v, step):
         late = (v + 3) // 6

time: 471 us -> 460 us (0.977); the launches traced: 464 us -> 459 us
  no operation moved by 1% of the time
where the time goes in v6:
time: 460 us; the launch traced here: 459 us
  Pallas kernels  458 us (100%)
    pallas_call x1, Pallas kernels, local_purify(): pl.pallas_call(main_kernel, out_shape=(jax.ShapeDtypeStruct((mats * G * G...  432 us
    pallas_call x1, Pallas kernels, local_purify(): pl.pallas_call(unpack_kernel, out_shape=(jax.ShapeDtypeStruct(ham.shape,...  26.2 us

profile of v6, /device:TPU:1, one launch (start us, length us, event | category | flops | bytes accessed | tf_op | source)
XLA Modules:
  0.0 459.4 jit_solution(9566295408908869640)
XLA Ops:
  0.6 431.7 %purify.1 = (f32[144,256,256]{2,1,0:T(8,128)}, f32[16,8,128]{2,1,0:T(8,128)}) custom-call(f32[2,16]{1,0:T(2,128)} %bitcast.1, s32[16]{0:T(128)} %occ.1, f32[16,768,768]{2,1,0:T(8,128)} %ham.1), custom_call_target="tpu_custom_call" | custom-call | flops 304405807104 | bytes 125829120 | tf_op jit(solution)/shard_map/purify/pallas_call | solution.py:575
  432.3 0.0 copy-start
  432.3 0.8 copy-done
  433.2 26.2 %unpack.1 = (f32[16,768,768]{2,1,0:T(8,128)}, f32[16]{0:T(128)}) custom-call(f32[144,256,256]{2,1,0:T(8,128)} %get-tuple-element.4.land, f32[16,8,128]{2,1,0:T(8,128)S(1)} %copy-done), custom_call_target="tpu_custom_call" | custom-call | flops 1000000 | bytes 78643200 | tf_op jit(solution)/shard_map/unpack/pallas_call | solution.py:606
Async XLA Ops:
  432.3 0.8 copy-start

commit v7 on v6

--- a/solution.py
+++ b/solution.py
@@ -78,8 +78,8 @@
 
 def main_kernel(
     bounds, occ, ham, land, ener,
-    buf_a, buf_b, buf_c, stage, sums, e_vec,
-    so_sem, r_sem, in_send, aid_sem, aid_send, land_sem, relay_sem, out_send, e_sem, e_send,
+    buf_a, buf_b, buf_c, stage, sums, e_vec, corner, t_vec, t_land,
+    so_sem, r_sem, corner_sem, t_sem, t_send, in_send, aid_sem, aid_send, land_sem, relay_sem, out_send, e_sem, e_send,
 ):
     tile = stage.shape[2]
     order = NB * tile
@@ -160,6 +160,17 @@
 
         return carry
 
+    quarter = tile // 2
+
+    @pl.when(differ == 0)
+    def _():
+        for e in range(2):
+            for i in range(NB):
+                spot = pl.ds(i * quarter, quarter)
+                pltpu.make_async_copy(
+                    ham.at[y * 4 + (1 - x) * 2 + 8 * e, spot, spot], corner.at[e, i], corner_sem.at[e]
+                ).start()
+
     lax.fori_loop(0, 5, send_in, 0)
 
     def wait_for(ref, sem):
@@ -168,6 +179,21 @@
     rows = lax.broadcasted_iota(jnp.int32, (tile, tile), 0)
     cols = lax.broadcasted_iota(jnp.int32, (tile, tile), 1)
     eye = jnp.where(rows == cols, 1.0, 0.0).astype(F32)
+
+    @pl.when(differ == 0)
+    def _():
+        for e in range(2):
+            wait_for(corner.at[e], corner_sem.at[e])
+            part = fold(corner[e, 0] * eye[:quarter, :quarter])
+            for i in range(1, NB):
+                part += fold(corner[e, i] * eye[:quarter, :quarter])
+            t_vec[e] = part
+        for e in range(2):
+            pltpu.make_async_remote_copy(
+                t_vec.at[e], t_land, t_send, t_sem,
+                device_id=device(y, 1 - x, e), device_id_type=MESH,
+            ).start()
+
 
     def send_out(rnd, row, col):
         mat = rnd * 8 + own
@@ -259,16 +285,14 @@
 
             lax.fori_loop(0, 2 * count, body, 0)
 
-        @pl.when((job == 2) & (c == 1) & (turn >= 12))
-        def _():
-            later = (turn - 11) // 2
-            low = differ * later * (2 * turn - 23)
-            relays(1, 0, low, differ * (3 - later) + (1 - differ) * (turn // 14))
-
-    def relay_last(rnd, v):
-        @pl.when((rnd == 1) & (c == 1) & (v >= 1) & (v < UPPER3 - 3 * differ))
-        def _():
-            relays(1, 0, v + 6 * differ, 1)
+        off = (differ == 1) & (turn >= 11) & (turn < 14)
+        far = (differ == 0) & (turn >= 13)
+
+        @pl.when((job == 2) & (c == 1) & (off | far))
+        def _():
+            nth = turn - 13 + 2 * differ
+            low = nth * (2 + nth // 2)
+            relays(1, 0, low, 2 + 2 * (nth % 2) + nth // 2)
 
     def tiles_of(turn):
         out = []
@@ -287,37 +311,68 @@
         col = base + (1 - half) * step + half * (1 + (step + 1) // 2)
         return row * late + v * (1 - late), col * late + (G + step) * (1 - late)
 
-    def send_aid(v):
-        for row, col, _ in tiles_of(v):
+    def near_tiles(turn):
+        return [(turn, turn, True), (turn // 2, 1 + (turn + 1) // 2, False)]
+
+    def other_tiles(turn):
+        off = [(turn, G + j, False) for j in range(G)]
+        off.append((G + turn // 2, G + 1 + (turn + 1) // 2, False))
+        return [*off, (G + turn, G + turn, True)]
+
+    def send_aid(tiles):
+        for row, col, _ in tiles:
             ref = stage.at[2, slot_of(row, col)]
             pltpu.make_async_remote_copy(
                 ref, ref, aid_send, aid_sem, device_id=device(y, x, 0), device_id_type=MESH
             ).start()
 
-    def square(src, job, before, may_aid):
+    def square_tiles(src, tiles, keep, early=False):
+        def cross(row, col):
+            part = chain(src, src, row, col, ((0, 2), (0, 1)))
+            return part + part.T
+
+        ready = [cross(row, col) if early and diag else None for row, col, diag in tiles]
+        for (row, col, diag), part in zip(tiles, ready):
+            if diag:
+                part = cross(row, col) if part is None else part
+                val = chain(src, src, row, col, ((1, 1), (0, 0))) + part
+            else:
+                val = chain(src, src, row, col, PASSES)
+            put(buf_b, row, col, val, diag)
+            if keep is not None:
+                stage[2, slot_of(row, col) * (1 - keep) + UPPER * keep] = val
+            sums[2] += fold(val * get(src, row, col)) * (1.0 if diag else 2.0)
+
+    def square_a(job, before, between):
         own_job = (job + 1) // 2
+        sums[2] = jnp.zeros_like(sums[2])
+
+        def near(v, carry):
+            pl.when((job == 0) & (v > 0))(lambda: send_aid(near_tiles(v - 1)))
+            square_tiles(buf_a, near_tiles(v), own_job)
+            return carry
+
+        def other(v, carry):
+            relay_early(job, before + v)
+            pl.when((job == 0) & (v == 0))(lambda: send_aid(near_tiles(2)))
+            pl.when((job == 0) & (v > 0))(lambda: send_aid(other_tiles(v - 1)))
+            square_tiles(buf_a, other_tiles(v), own_job, True)
+            return carry
+
+        lax.fori_loop(0, 3, near, 0)
+        between()
+        lax.fori_loop(0, 3, other, 0)
+        pl.when(job == 0)(lambda: send_aid(other_tiles(2)))
+
+    def square_c(job, before):
+        sums[2] = jnp.zeros_like(sums[2])
 
         def turn(v, carry):
             relay_early(job, before + v)
-            if may_aid:
-                pl.when((job == 0) & (v > 0))(lambda: send_aid(v - 1))
-            for row, col, diag in tiles_of(v):
-                if diag:
-                    cross = chain(src, src, row, col, ((0, 2), (0, 1)))
-                    val = chain(src, src, row, col, ((1, 1), (0, 0)))
-                    val = val + (cross + cross.T)
-                else:
-                    val = chain(src, src, row, col, PASSES)
-                put(buf_b, row, col, val, diag)
-                if may_aid:
-                    stage[2, slot_of(row, col) * (1 - own_job) + UPPER * own_job] = val
-                sums[2] += fold(val * get(src, row, col)) * (1.0 if diag else 2.0)
+            square_tiles(buf_c, tiles_of(v), None)
             return carry
 
-        sums[2] = jnp.zeros_like(sums[2])
         lax.fori_loop(0, 3, turn, 0)
-        if may_aid:
-            pl.when(job == 0)(lambda: send_aid(2))
 
     def absorb():
         wait_for(stage.at[2, pl.ds(0, UPPER)], aid_sem)
@@ -371,8 +426,6 @@
             def _():
                 for step in range(3):
                     send_out(rnd, *unit(v - 1, step))
-
-            relay_last(rnd, v)
 
             for step in range(3):
                 row, col = unit(v, step)
@@ -397,15 +450,30 @@
         put_in = (job + 2) % 3
         mat = own_job * (rnd * 8 + own) + (1 - own_job) * (8 + own - 1)
         wait_for(stage.at[put_in, pl.ds(0, 15)], so_sem.at[put_in])
-        wait_for(stage.at[put_in, pl.ds(15, 6), pl.ds(0, tile * 7 // 8)], r_sem.at[put_in])
-        half = tile // 2
-        for i in range(G, NB):
-            slot = slot_of(i, i)
-            stage[put_in, slot, half:, :half] = stage[put_in, slot, :half, half:].T
+        starts = job == 1 - c
+
+        def far_block():
+            wait_for(stage.at[put_in, pl.ds(15, 6), pl.ds(0, tile * 7 // 8)], r_sem.at[put_in])
+            for i in range(G, NB):
+                slot = slot_of(i, i)
+                stage[put_in, slot, quarter:, :quarter] = stage[put_in, slot, :quarter, quarter:].T
+
+        @pl.when(starts)
+        def _():
+            wait_for(t_land, t_sem)
+
+        @pl.when(~starts)
+        def _():
+            far_block()
+            part = fold(stage[put_in, slot_of(G, G)] * eye)
+            for i in range(G + 1, NB):
+                part += fold(stage[put_in, slot_of(i, i)] * eye)
+            t_land[...] = part[:, :quarter] + part[:, quarter:]
+
         diag_sum = fold(stage[put_in, slot_of(0, 0)] * eye)
-        for i in range(1, NB):
+        for i in range(1, G):
             diag_sum += fold(stage[put_in, slot_of(i, i)] * eye)
-        mean = total(diag_sum) / order
+        mean = (total(diag_sum) + total(t_land[...])) / order
         filled = occ[mat].astype(F32)
         scale = jnp.minimum(
             filled / (bounds[1, mat] - mean), (order - filled) / (mean - bounds[0, mat])
@@ -414,7 +482,8 @@
         slope = scale / order
         sums[0:2] = jnp.zeros_like(sums[0:2])
 
-        def first(v, c_):
+        def first(q, c_):
+            v = q + 2 * (q // 3 - q // 6) - 4 * (q // 5)
             for step in range(3):
                 row, col = unit(v, step)
                 one = jnp.where(row == col, 1.0, 0.0)
@@ -424,17 +493,23 @@
                 sums[1] += fold(val * val) * (2.0 - one)
             return c_
 
-        lax.fori_loop(0, 7, first, 0)
+        lax.fori_loop(0, 5 + 2 * jnp.where(starts, 0, 1), first, 0)
         given = (job == 2) & (c == 0)
         mine = job > 0
 
         def step(s, c_):
             @pl.when(((s == 0) & ~given) | ((s == 2) & mine))
             def _():
-                square(buf_a, job, 6 * s, True)
+                def between():
+                    @pl.when(starts & (s == 0))
+                    def _():
+                        far_block()
+                        lax.fori_loop(5, 7, first, 0)
+
+                square_a(job, 6 * s, between)
 
             pl.when((s == 0) & given)(absorb)
-            pl.when((s == 1) & mine)(lambda: square(buf_c, job, 6, False))
+            pl.when((s == 1) & mine)(lambda: square_c(job, 6))
             pl.when((s == 0) & mine)(lambda: cube(buf_a, buf_c, job, 3))
             pl.when((s == 1) & mine)(lambda: cube(buf_c, buf_a, job, 9))
             pl.when((s == 2) & mine)(lambda: finish(rnd, mat))
@@ -473,6 +548,7 @@
     def _():
         pl.when(c == 0)(lambda: wait_tiles(105 + 72, in_send))
         pl.when(c == 1)(lambda: wait_tiles(105 + 48, in_send))
+        wait_for(t_vec, t_send)
         wait_tiles(4 * 96, out_send)
         wait_tiles(4 * 63, land_sem)
 
@@ -585,8 +661,14 @@
                 pltpu.VMEM((3, UPPER + 1, tile, tile), F32),
                 pltpu.VMEM((3, 8, tile), F32),
                 pltpu.VMEM((2, 8, 128), F32),
+                pltpu.VMEM((2, NB, tile // 2, tile // 2), F32),
+                pltpu.VMEM((2, 8, tile // 2), F32),
+                pltpu.VMEM((8, tile // 2), F32),
                 pltpu.SemaphoreType.DMA((3,)),
                 pltpu.SemaphoreType.DMA((3,)),
+                pltpu.SemaphoreType.DMA((2,)),
+                pltpu.SemaphoreType.DMA,
+                pltpu.SemaphoreType.DMA,
                 pltpu.SemaphoreType.DMA,
                 pltpu.SemaphoreType.DMA,
                 pltpu.SemaphoreType.DMA,

time: 460 us -> 532 us (1.16)
  Pallas kernels: 458 us -> 529 us
    pallas_call x1, Pallas kernels: 432 us -> 503 us  [local_purify(): pl.pallas_call(main_kernel, out_shape=(jax.ShapeDtypeStruct((mats * G * G...]
where the time goes in v7:
time: 532 us; the launch traced here: 530 us
  Pallas kernels  529 us (99%)
    pallas_call x1, Pallas kernels, local_purify(): pl.pallas_call(main_kernel, out_shape=(jax.ShapeDtypeStruct((mats * G * G...  503 us
    pallas_call x1, Pallas kernels, local_purify(): pl.pallas_call(unpack_kernel, out_shape=(jax.ShapeDtypeStruct(ham.shape,...  26.2 us

profile of v7, /device:TPU:1, one launch (start us, length us, event | category | flops | bytes accessed | tf_op | source)
XLA Modules:
  0.0 530.3 jit_solution(16964822886839925044)
XLA Ops:
  0.6 502.6 %purify.1 = (f32[144,256,256]{2,1,0:T(8,128)}, f32[16,8,128]{2,1,0:T(8,128)}) custom-call(f32[2,16]{1,0:T(2,128)} %bitcast.1, s32[16]{0:T(128)} %occ.1, f32[16,768,768]{2,1,0:T(8,128)} %ham.1), custom_call_target="tpu_custom_call" | custom-call | flops 304405807104 | bytes 125829120 | tf_op jit(solution)/shard_map/purify/pallas_call | solution.py:651
  503.2 0.0 copy-start
  503.3 0.8 copy-done
  504.1 26.2 %unpack.1 = (f32[16,768,768]{2,1,0:T(8,128)}, f32[16]{0:T(128)}) custom-call(f32[144,256,256]{2,1,0:T(8,128)} %get-tuple-element.4.land, f32[16,8,128]{2,1,0:T(8,128)S(1)} %copy-done), custom_call_target="tpu_custom_call" | custom-call | flops 1000000 | bytes 78643200 | tf_op jit(solution)/shard_map/unpack/pallas_call | solution.py:688
Async XLA Ops:
  503.2 0.8 copy-start

commit v8 on v7

--- a/solution.py
+++ b/solution.py
@@ -90,6 +90,14 @@
     def device(dy, dx, cd):
         return {'depth': dy, 'row': dx, 'col': cd}
 
+    def wait_for(ref, sem):
+        pltpu.make_async_copy(ref, ref, sem).wait()
+
+    quarter = tile // 2
+    rows = lax.broadcasted_iota(jnp.int32, (tile, tile), 0)
+    cols = lax.broadcasted_iota(jnp.int32, (tile, tile), 1)
+    eye = jnp.where(rows == cols, 1.0, 0.0).astype(F32)
+
     barrier = pltpu.get_barrier_semaphore()
     for k in range(1, 8):
         pl.semaphore_signal(
@@ -97,7 +105,31 @@
             device_id=device(flip(y, k // 4), flip(x, (k // 2) % 2), flip(c, k % 2)),
             device_id_type=MESH,
         )
+
+    @pl.when(differ == 0)
+    def _():
+        for e in range(2):
+            for i in range(NB):
+                spot = pl.ds(i * quarter, quarter)
+                pltpu.make_async_copy(
+                    ham.at[y * 4 + (1 - x) * 2 + 8 * e, spot, spot], corner.at[e, i], corner_sem.at[e]
+                ).start()
+        for e in range(2):
+            wait_for(corner.at[e], corner_sem.at[e])
+            part = fold(corner[e, 0] * eye[:quarter, :quarter])
+            for i in range(1, NB):
+                part += fold(corner[e, i] * eye[:quarter, :quarter])
+            t_vec[e] = part
+
     pl.semaphore_wait(barrier, 7)
+
+    @pl.when(differ == 0)
+    def _():
+        for e in range(2):
+            pltpu.make_async_remote_copy(
+                t_vec.at[e], t_land, t_send, t_sem,
+                device_id=device(y, 1 - x, e), device_id_type=MESH,
+            ).start()
 
     def h_tile(mat, i, j):
         return ham.at[mat, pl.ds(i * tile, tile), pl.ds(j * tile, tile)]
@@ -160,40 +192,7 @@
 
         return carry
 
-    quarter = tile // 2
-
-    @pl.when(differ == 0)
-    def _():
-        for e in range(2):
-            for i in range(NB):
-                spot = pl.ds(i * quarter, quarter)
-                pltpu.make_async_copy(
-                    ham.at[y * 4 + (1 - x) * 2 + 8 * e, spot, spot], corner.at[e, i], corner_sem.at[e]
-                ).start()
-
     lax.fori_loop(0, 5, send_in, 0)
-
-    def wait_for(ref, sem):
-        pltpu.make_async_copy(ref, ref, sem).wait()
-
-    rows = lax.broadcasted_iota(jnp.int32, (tile, tile), 0)
-    cols = lax.broadcasted_iota(jnp.int32, (tile, tile), 1)
-    eye = jnp.where(rows == cols, 1.0, 0.0).astype(F32)
-
-    @pl.when(differ == 0)
-    def _():
-        for e in range(2):
-            wait_for(corner.at[e], corner_sem.at[e])
-            part = fold(corner[e, 0] * eye[:quarter, :quarter])
-            for i in range(1, NB):
-                part += fold(corner[e, i] * eye[:quarter, :quarter])
-            t_vec[e] = part
-        for e in range(2):
-            pltpu.make_async_remote_copy(
-                t_vec.at[e], t_land, t_send, t_sem,
-                device_id=device(y, 1 - x, e), device_id_type=MESH,
-            ).start()
-
 
     def send_out(rnd, row, col):
         mat = rnd * 8 + own

time: 532 us -> 460 us (0.86)
  Pallas kernels: 529 us -> 457 us
    pallas_call x1, Pallas kernels: 503 us -> 430 us  [local_purify(): pl.pallas_call(main_kernel, out_shape=(jax.ShapeDtypeStruct((mats * G * G...]
where the time goes in v8:
time: 460 us; the launch traced here: 458 us
  Pallas kernels  457 us (99%)
    pallas_call x1, Pallas kernels, local_purify(): pl.pallas_call(main_kernel, out_shape=(jax.ShapeDtypeStruct((mats * G * G...  430 us
    pallas_call x1, Pallas kernels, local_purify(): pl.pallas_call(unpack_kernel, out_shape=(jax.ShapeDtypeStruct(ham.shape,...  26.2 us

profile of v8, /device:TPU:1, one launch (start us, length us, event | category | flops | bytes accessed | tf_op | source)
XLA Modules:
  0.0 458.0 jit_solution(268851566162928758)
XLA Ops:
  0.6 430.3 %purify.1 = (f32[144,256,256]{2,1,0:T(8,128)}, f32[16,8,128]{2,1,0:T(8,128)}) custom-call(f32[2,16]{1,0:T(2,128)} %bitcast.1, s32[16]{0:T(128)} %occ.1, f32[16,768,768]{2,1,0:T(8,128)} %ham.1), custom_call_target="tpu_custom_call" | custom-call | flops 304405807104 | bytes 125829120 | tf_op jit(solution)/shard_map/purify/pallas_call | solution.py:650
  430.9 0.0 copy-start
  430.9 0.8 copy-done
  431.8 26.2 %unpack.1 = (f32[16,768,768]{2,1,0:T(8,128)}, f32[16]{0:T(128)}) custom-call(f32[144,256,256]{2,1,0:T(8,128)} %get-tuple-element.4.land, f32[16,8,128]{2,1,0:T(8,128)S(1)} %copy-done), custom_call_target="tpu_custom_call" | custom-call | flops 1000000 | bytes 78643200 | tf_op jit(solution)/shard_map/unpack/pallas_call | solution.py:687
Async XLA Ops:
  430.9 0.8 copy-start

commit v9 on v8

--- a/solution.py
+++ b/solution.py
@@ -284,14 +284,12 @@
 
             lax.fori_loop(0, 2 * count, body, 0)
 
-        off = (differ == 1) & (turn >= 11) & (turn < 14)
-        far = (differ == 0) & (turn >= 13)
-
-        @pl.when((job == 2) & (c == 1) & (off | far))
-        def _():
-            nth = turn - 13 + 2 * differ
-            low = nth * (2 + nth // 2)
-            relays(1, 0, low, 2 + 2 * (nth % 2) + nth // 2)
+        @pl.when((job == 2) & (c == 1) & (turn >= 11) & (turn < 13 + differ))
+        def _():
+            nth = turn - 11
+            low = differ * (3 * nth - nth // 2) + (1 - differ) * 2 * nth
+            count = differ * (3 - nth + 3 * (nth // 2)) + (1 - differ) * (2 + 2 * nth)
+            relays(1, 0, low, count)
 
     def tiles_of(turn):
         out = []
@@ -420,14 +418,18 @@
         co = coefs()
         sums[0] = jnp.zeros_like(sums[0])
 
+        def when(v):
+            pair = (v + 1) // 2 % 3
+            return v + pair * (5 - 3 * pair)
+
         def turn(v, carry):
             @pl.when(v > 0)
             def _():
                 for step in range(3):
-                    send_out(rnd, *unit(v - 1, step))
+                    send_out(rnd, *unit(when(v - 1), step))
 
             for step in range(3):
-                row, col = unit(v, step)
+                row, col = unit(when(v), step)
                 val = combine(src, row, col, co)
                 slot = slot_of(row, col)
                 weight = jnp.where(row == col, 1.0, 2.0)
@@ -437,7 +439,7 @@
 
         lax.fori_loop(0, 7, turn, 0)
         for step in range(3):
-            send_out(rnd, *unit(6, step))
+            send_out(rnd, *unit(when(6), step))
 
     def one_job(job, carry):
         pl.when((job > 0) | (c == 1))(lambda: run_job(job))

time: 460 us -> 457 us (level)
  no operation moved by 1% of the time
where the time goes in v9:
time: 457 us
  Pallas kernels  455 us (100%)
    pallas_call x1, Pallas kernels, local_purify(): pl.pallas_call(main_kernel, out_shape=(jax.ShapeDtypeStruct((mats * G * G...  429 us
    pallas_call x1, Pallas kernels, local_purify(): pl.pallas_call(unpack_kernel, out_shape=(jax.ShapeDtypeStruct(ham.shape,...  26.2 us

profile of v9, /device:TPU:1, one launch (start us, length us, event | category | flops | bytes accessed | tf_op | source)
XLA Modules:
  0.0 456.8 jit_solution(14632134820208423030)
XLA Ops:
  0.6 429.1 %purify.1 = (f32[144,256,256]{2,1,0:T(8,128)}, f32[16,8,128]{2,1,0:T(8,128)}) custom-call(f32[2,16]{1,0:T(2,128)} %bitcast.1, s32[16]{0:T(128)} %occ.1, f32[16,768,768]{2,1,0:T(8,128)} %ham.1), custom_call_target="tpu_custom_call" | custom-call | flops 304405807104 | bytes 125829120 | tf_op jit(solution)/shard_map/purify/pallas_call | solution.py:652
  429.7 0.0 copy-start
  429.7 0.8 copy-done
  430.6 26.2 %unpack.1 = (f32[16,768,768]{2,1,0:T(8,128)}, f32[16]{0:T(128)}) custom-call(f32[144,256,256]{2,1,0:T(8,128)} %get-tuple-element.4.land, f32[16,8,128]{2,1,0:T(8,128)S(1)} %copy-done), custom_call_target="tpu_custom_call" | custom-call | flops 1000000 | bytes 78643200 | tf_op jit(solution)/shard_map/unpack/pallas_call | solution.py:689
Async XLA Ops:
  429.7 0.8 copy-start

commit v10 on v9

--- a/solution.py
+++ b/solution.py
@@ -12,7 +12,7 @@
 NB = 2 * G
 UPPER = NB * (NB + 1) // 2
 UPPER3 = G * (G + 1) // 2
-OVER_X = 8
+OVER_X = 7
 F32 = jnp.float32
 BF16 = jnp.bfloat16
 PASSES = ((0, 2), (2, 0), (1, 1), (0, 1), (1, 0), (0, 0))
@@ -340,26 +340,30 @@
                 stage[2, slot_of(row, col) * (1 - keep) + UPPER * keep] = val
             sums[2] += fold(val * get(src, row, col)) * (1.0 if diag else 2.0)
 
-    def square_a(job, before, between):
-        own_job = (job + 1) // 2
+    def square_a(job, before, between, given):
+        keep = (job + 1) // 2 * jnp.where(given, 0, 1)
+        aid = job == 0
         sums[2] = jnp.zeros_like(sums[2])
 
         def near(v, carry):
-            pl.when((job == 0) & (v > 0))(lambda: send_aid(near_tiles(v - 1)))
-            square_tiles(buf_a, near_tiles(v), own_job)
+            pl.when(aid & (v > 1))(lambda: send_aid(near_tiles(v - 1)))
+            square_tiles(buf_a, near_tiles(v), keep)
             return carry
 
         def other(v, carry):
             relay_early(job, before + v)
-            pl.when((job == 0) & (v == 0))(lambda: send_aid(near_tiles(2)))
-            pl.when((job == 0) & (v > 0))(lambda: send_aid(other_tiles(v - 1)))
-            square_tiles(buf_a, other_tiles(v), own_job, True)
+            pl.when(aid & (v == 0))(lambda: send_aid(near_tiles(2)))
+            pl.when(aid & (v > 0))(lambda: send_aid(other_tiles(v - 1)))
+            square_tiles(buf_a, other_tiles(v), keep)
             return carry
 
-        lax.fori_loop(0, 3, near, 0)
+        lax.fori_loop(jnp.where(aid, 1, 0), jnp.where(given, 1, 3), near, 0)
         between()
-        lax.fori_loop(0, 3, other, 0)
-        pl.when(job == 0)(lambda: send_aid(other_tiles(2)))
+
+        @pl.when(~given)
+        def _():
+            lax.fori_loop(0, 3, other, 0)
+            pl.when(aid)(lambda: send_aid(other_tiles(2)))
 
     def square_c(job, before):
         sums[2] = jnp.zeros_like(sums[2])
@@ -372,7 +376,7 @@
         lax.fori_loop(0, 3, turn, 0)
 
     def absorb():
-        wait_for(stage.at[2, pl.ds(0, UPPER)], aid_sem)
+        wait_for(stage.at[2, pl.ds(0, UPPER - 2)], aid_sem)
         sums[2] = jnp.zeros_like(sums[2])
 
         def turn(v, carry):
@@ -499,7 +503,7 @@
         mine = job > 0
 
         def step(s, c_):
-            @pl.when(((s == 0) & ~given) | ((s == 2) & mine))
+            @pl.when((s == 0) | ((s == 2) & mine))
             def _():
                 def between():
                     @pl.when(starts & (s == 0))
@@ -507,7 +511,7 @@
                         far_block()
                         lax.fori_loop(5, 7, first, 0)
 
-                square_a(job, 6 * s, between)
+                square_a(job, 6 * s, between, given & (s == 0))
 
             pl.when((s == 0) & given)(absorb)
             pl.when((s == 1) & mine)(lambda: square_c(job, 6))
@@ -543,7 +547,7 @@
 
     @pl.when(c == 1)
     def _():
-        wait_for(stage.at[2, pl.ds(0, UPPER)], aid_send)
+        wait_for(stage.at[2, pl.ds(0, UPPER - 2)], aid_send)
 
     @pl.when(differ == 0)
     def _():
@@ -562,83 +566,104 @@
 
 
 RING = 4
-
-
-def unpack_kernel(land, ener, out, energy, held, block, in_sem, out_sem):
+ROW_RING = 10
+
+
+def ring(count, depth, load, store, work):
+    def prime(unit, carry):
+        load(unit, lambda copy: copy.start())
+        return carry
+
+    def turn(unit, carry):
+        load(unit, None)
+        pl.when(unit >= depth)(lambda: store(unit - depth).wait())
+        work(unit)
+        store(unit).start()
+        pl.when(unit + depth < count)(lambda: load(unit + depth, lambda copy: copy.start()))
+        return carry
+
+    def drain(unit, carry):
+        store(unit).wait()
+        return carry
+
+    lax.fori_loop(0, depth, prime, 0)
+    lax.fori_loop(0, count, turn, 0)
+    lax.fori_loop(count - depth, count, drain, 0)
+
+
+def unpack_kernel(land, ener, out, energy, held, block, row_held, row_block, in_sem, out_sem, row_in, row_out):
     mats, tile = out.shape[0], land.shape[1]
     half = tile // 2
     x, c = lax.axis_index('row'), lax.axis_index('col')
     differ = flip(x, c)
+    energy[...] = jnp.sum(ener[...], axis=0)[0, : energy.shape[0]]
 
     def load(mat, act):
         slot = mat % RING
-        for kind, count in ((0, UPPER3), (1, G * G)):
-
-            @pl.when(differ == kind)
-            def _():
-                act(
-                    pltpu.make_async_copy(
-                        land.at[pl.ds(mat * count, count)],
-                        held.at[slot, pl.ds(0, count)],
-                        in_sem.at[slot],
-                    )
-                )
+        copy = pltpu.make_async_copy(
+            land.at[pl.ds(mat * UPPER3, UPPER3)], held.at[slot], in_sem.at[slot]
+        )
+        copy.wait() if act is None else act(copy)
 
     def store(mat):
         slot = mat % RING
         return pltpu.make_async_copy(block.at[slot], out.at[mat], out_sem.at[slot])
 
-    def prime(mat, carry):
-        load(mat, lambda copy: copy.start())
-        return carry
-
-    lax.fori_loop(0, RING, prime, 0)
-    energy[...] = jnp.sum(ener[...], axis=0)[0, : energy.shape[0]]
-
-    def turn(mat, carry):
+    def mirror(mat):
         slot = mat % RING
-        turned = flip((mat // 2) % 2, x)
-        load(mat, lambda copy: copy.wait())
-        pl.when(mat >= RING)(lambda: store(mat - RING).wait())
 
         def write(i, j, val):
             rows, cols = val.shape
             block[slot, pl.ds(i * half, rows), pl.ds(j * half, cols)] = val
 
-        @pl.when(differ == 0)
-        def _():
-            for i in range(G):
-                for j in range(i, G):
-                    place = slot3_of(i, j)
-                    if i == j:
-                        top = held[slot, place, :half, :]
-                        write(2 * i, 2 * i, top)
-                        write(2 * i + 1, 2 * i, top[:, half:].T)
-                        write(2 * i + 1, 2 * i + 1, held[slot, place, half:, half:])
-                    else:
-                        val = held[slot, place]
-                        write(2 * i, 2 * j, val)
-                        write(2 * j, 2 * i, val.T)
-
-        @pl.when(differ * (1 - turned) == 1)
-        def _():
-            for i in range(G):
-                for j in range(G):
-                    write(2 * i, 2 * j, held[slot, i * G + j])
-
-        @pl.when(differ * turned == 1)
-        def _():
-            for i in range(G):
-                for j in range(G):
-                    write(2 * j, 2 * i, held[slot, i * G + j].T)
-
-        store(mat).start()
-        pl.when(mat + RING < mats)(lambda: load(mat + RING, lambda copy: copy.start()))
-        return carry
-
-    lax.fori_loop(0, mats, turn, 0)
-    for mat in range(mats - RING, mats):
-        store(mat).wait()
+        for i in range(G):
+            for j in range(i, G):
+                place = slot3_of(i, j)
+                if i == j:
+                    top = held[slot, place, :half, :]
+                    write(2 * i, 2 * i, top)
+                    write(2 * i + 1, 2 * i, top[:, half:].T)
+                    write(2 * i + 1, 2 * i + 1, held[slot, place, half:, half:])
+                else:
+                    val = held[slot, place]
+                    write(2 * i, 2 * j, val)
+                    write(2 * j, 2 * i, val.T)
+
+    def turned(mat):
+        return flip((mat // 2) % 2, x)
+
+    def load_row(unit, act):
+        slot, mat, row = unit % ROW_RING, unit // G, unit % G
+        if act is None:
+            pltpu.make_async_copy(row_held.at[slot], row_held.at[slot], row_in.at[slot]).wait()
+            return
+        flipped = turned(mat)
+        for k in range(G):
+            place = (1 - flipped) * (row * G + k) + flipped * (k * G + row)
+            act(pltpu.make_async_copy(land.at[mat * G * G + place], row_held.at[slot, k], row_in.at[slot]))
+
+    def store_row(unit):
+        slot, mat, row = unit % ROW_RING, unit // G, unit % G
+        return pltpu.make_async_copy(
+            row_block.at[slot], out.at[mat, pl.ds(row * tile, tile), :], row_out.at[slot]
+        )
+
+    def turn_row(unit):
+        slot = unit % ROW_RING
+        flipped = turned(unit // G)
+
+        @pl.when(flipped == 0)
+        def _():
+            for k in range(G):
+                row_block[slot, :, pl.ds(k * tile, tile)] = row_held[slot, k]
+
+        @pl.when(flipped == 1)
+        def _():
+            for k in range(G):
+                row_block[slot, :, pl.ds(k * tile, tile)] = row_held[slot, k].T
+
+    pl.when(differ == 0)(lambda: ring(mats, RING, load, store, mirror))
+    pl.when(differ == 1)(lambda: ring(mats * G, ROW_RING, load_row, store_row, turn_row))
 
 
 def solution(mesh):
@@ -695,10 +720,14 @@
             in_specs=[any_spec, pl.BlockSpec(memory_space=pltpu.VMEM)],
             out_specs=(any_spec, pl.BlockSpec(memory_space=pltpu.VMEM)),
             scratch_shapes=[
-                pltpu.VMEM((RING, G * G, tile, tile), F32),
+                pltpu.VMEM((RING, UPPER3, tile, tile), F32),
                 pltpu.VMEM((RING, blk, blk), F32),
+                pltpu.VMEM((ROW_RING, G, tile, tile), F32),
+                pltpu.VMEM((ROW_RING, tile, blk), F32),
                 pltpu.SemaphoreType.DMA((RING,)),
                 pltpu.SemaphoreType.DMA((RING,)),
+                pltpu.SemaphoreType.DMA((ROW_RING,)),
+                pltpu.SemaphoreType.DMA((ROW_RING,)),
             ],
             compiler_params=pltpu.CompilerParams(vmem_limit_bytes=40 * 2**20),
             cost_estimate=pl.CostEstimate(flops=10**6, bytes_accessed=75 * 2**20, transcendentals=0),

time: 457 us -> 458 us (level)
  no operation moved by 1% of the time
where the time goes in v10:
time: 458 us; the launch traced here: 457 us
  Pallas kernels  456 us (100%)
    pallas_call x1, Pallas kernels, local_purify(): pl.pallas_call(main_kernel, out_shape=(jax.ShapeDtypeStruct((mats * G * G...  430 us
    pallas_call x1, Pallas kernels, local_purify(): pl.pallas_call(unpack_kernel, out_shape=(jax.ShapeDtypeStruct(ham.shape,...  25.5 us

profile of v10, /device:TPU:1, one launch (start us, length us, event | category | flops | bytes accessed | tf_op | source)
XLA Modules:
  0.0 457.3 jit_solution(15464841691077790939)
XLA Ops:
  0.6 430.4 %purify.1 = (f32[144,256,256]{2,1,0:T(8,128)}, f32[16,8,128]{2,1,0:T(8,128)}) custom-call(f32[2,16]{1,0:T(2,128)} %bitcast.1, s32[16]{0:T(128)} %occ.1, f32[16,768,768]{2,1,0:T(8,128)} %ham.1), custom_call_target="tpu_custom_call" | custom-call | flops 304405807104 | bytes 125829120 | tf_op jit(solution)/shard_map/purify/pallas_call | solution.py:677
  431.0 0.0 copy-start
  431.0 0.8 copy-done
  431.9 25.5 %unpack.1 = (f32[16,768,768]{2,1,0:T(8,128)}, f32[16]{0:T(128)}) custom-call(f32[144,256,256]{2,1,0:T(8,128)} %get-tuple-element.4.land, f32[16,8,128]{2,1,0:T(8,128)S(1)} %copy-done), custom_call_target="tpu_custom_call" | custom-call | flops 1000000 | bytes 78643200 | tf_op jit(solution)/shard_map/unpack/pallas_call | solution.py:714
Async XLA Ops:
  431.0 0.8 copy-start

commit v11 on v10

--- a/solution.py
+++ b/solution.py
@@ -284,12 +284,11 @@
 
             lax.fori_loop(0, 2 * count, body, 0)
 
-        @pl.when((job == 2) & (c == 1) & (turn >= 11) & (turn < 13 + differ))
-        def _():
-            nth = turn - 11
+        @pl.when((job == 2) & (c == 1) & (turn >= 12))
+        def _():
+            nth = turn - 12
             low = differ * (3 * nth - nth // 2) + (1 - differ) * 2 * nth
-            count = differ * (3 - nth + 3 * (nth // 2)) + (1 - differ) * (2 + 2 * nth)
-            relays(1, 0, low, count)
+            relays(1, 0, low, differ * (3 - (nth + 1) // 2) + (1 - differ) * 2)
 
     def tiles_of(turn):
         out = []
@@ -431,6 +430,10 @@
             def _():
                 for step in range(3):
                     send_out(rnd, *unit(when(v - 1), step))
+
+            @pl.when((rnd == 1) & (c * differ == 1) & (v >= 1) & (v < 3))
+            def _():
+                relays(1, 0, v + 6, 1)
 
             for step in range(3):
                 row, col = unit(when(v), step)

time: 458 us -> 458 us (level)
  no operation moved by 1% of the time
where the time goes in v11:
time: 458 us; the launch traced here: 457 us
  Pallas kernels  456 us (100%)
    pallas_call x1, Pallas kernels, local_purify(): pl.pallas_call(main_kernel, out_shape=(jax.ShapeDtypeStruct((mats * G * G...  430 us
    pallas_call x1, Pallas kernels, local_purify(): pl.pallas_call(unpack_kernel, out_shape=(jax.ShapeDtypeStruct(ham.shape,...  25.5 us

profile of v11, /device:TPU:1, one launch (start us, length us, event | category | flops | bytes accessed | tf_op | source)
XLA Modules:
  0.0 457.3 jit_solution(3604575878128956231)
XLA Ops:
  0.6 430.4 %purify.1 = (f32[144,256,256]{2,1,0:T(8,128)}, f32[16,8,128]{2,1,0:T(8,128)}) custom-call(f32[2,16]{1,0:T(2,128)} %bitcast.1, s32[16]{0:T(128)} %occ.1, f32[16,768,768]{2,1,0:T(8,128)} %ham.1), custom_call_target="tpu_custom_call" | custom-call | flops 304405807104 | bytes 125829120 | tf_op jit(solution)/shard_map/purify/pallas_call | solution.py:680
  431.0 0.0 copy-start
  431.0 0.8 copy-done
  431.9 25.5 %unpack.1 = (f32[16,768,768]{2,1,0:T(8,128)}, f32[16]{0:T(128)}) custom-call(f32[144,256,256]{2,1,0:T(8,128)} %get-tuple-element.4.land, f32[16,8,128]{2,1,0:T(8,128)S(1)} %copy-done), custom_call_target="tpu_custom_call" | custom-call | flops 1000000 | bytes 78643200 | tf_op jit(solution)/shard_map/unpack/pallas_call | solution.py:717
Async XLA Ops:
  431.0 0.8 copy-start
